TPU v7x, 256 devices: a whole 4x4x8 slice. The times are simulated.
256 devices in a mesh: section: 8 (over x, core), sp: 32 (over y, z).
Axes of the slice: x: 4, y: 4, z: 8, core: 2. Of those that a mesh axis runs over, the one named last changes fastest.
Arguments:
- field_in: bfloat16 [8, 384, 192, 768], P('section', 'sp'), may hold values from -6 to 6
- spectral_gain: bfloat16 [8, 192], P('section'), may hold values from 0.5 to 1.5
- spectral_weight: bfloat16 [8, 384, 192, 384], P('section', 'sp'), may hold values from -0.3125 to 0.3125
- mixer_gain: bfloat16 [8, 192], P('section'), may hold values from 0.5 to 1.5
- up_weight: bfloat16 [8, 192, 384], P('section'), may hold values from -0.4375 to 0.4375
- up_bias: bfloat16 [8, 384], P('section'), may hold values from -3 to 3
- down_weight: bfloat16 [8, 192, 384], P('section'), may hold values from -0.3125 to 0.3125
Outputs:
- next_field: bfloat16 [8, 384, 192, 768], P('section', 'sp')
All inputs are finite; a program needn't handle non-finite values.
Results may differ from a plain program's by a relative error of at most 0.012.
Values may be sent and summed in bfloat16 or wider, within the bound.
No kernel may reach another device: no remote copies, remote signals or barrier semaphores. Data moves between devices by JAX's collectives and lax.ppermute only.
A program may use at most 128 MiB of HBM per device.

v0:
```python
import math

import jax
import jax.numpy as jnp
from jax import lax
from jax.sharding import PartitionSpec as P

C = 192
NLAT = 384
NLON = 768
LMAX = 384
MMAX = 384


EPSILON = 1e-05


def passed_along(value, axis, by):
    count = lax.axis_size(axis)
    return lax.ppermute(value, axis, [(i, (i + by) % count) for i in range(count)])


def quad_weights(cycle_index, cycle_count):
    terms_count = cycle_count // 2
    orders = jnp.arange(1, terms_count + 1, dtype=jnp.int32)
    phase_turns = orders[None, :] * (2 * cycle_index[:, None] + 1) % (2 * cycle_count)
    angles = math.pi * phase_turns.astype(jnp.float32) / cycle_count
    orders_real = orders.astype(jnp.float32)
    series = jnp.sum(jnp.cos(angles) / (4.0 * orders_real * orders_real - 1.0)[None, :], axis=1)
    return 2.0 / cycle_count * (1.0 - 2.0 * series)


def fourier_tables(point_count, orders):
    points = jnp.arange(point_count, dtype=jnp.int32)
    phase_turns = points[:, None] * orders[None, :] % point_count
    angles = 2.0 * math.pi / point_count * phase_turns.astype(jnp.float32)
    cosines = jnp.cos(angles)
    sine_values = jnp.sin(angles)
    forward = jnp.stack([cosines, -sine_values], axis=1).astype(jnp.bfloat16)
    doubling = jnp.where(orders == 0, 1.0, 2.0).astype(jnp.float32)[:, None]
    inverse = jnp.stack([cosines.T * doubling, -sine_values.T * doubling], axis=0).astype(
        jnp.bfloat16
    )
    return (forward, inverse)


def step_entries(degree, order_col, cosines):
    active = degree >= order_col + 1.0
    further = degree >= order_col + 2.0
    degree_sq = degree * degree
    order_sq = order_col * order_col
    lead_coeff = jnp.sqrt(
        jnp.where(
            active, (4.0 * degree_sq - 1.0) / jnp.where(active, degree_sq - order_sq, 1.0), 0.0
        )
    )
    before = degree - 1.0
    before_sq = before * before
    trail_coeff = jnp.sqrt(
        jnp.where(
            further, (before_sq - order_sq) / jnp.where(further, 4.0 * before_sq - 1.0, 1.0), 0.0
        )
    )
    diag_top = jnp.where(active, lead_coeff * cosines, 1.0)
    off_top = jnp.where(active, -lead_coeff * trail_coeff, 0.0)
    off_low = jnp.where(active, 1.0, 0.0)
    diag_low = jnp.where(active, 0.0, 1.0)
    return (diag_top, off_top, off_low, diag_low)


def legendre_rows(order_index, cycle_count, degree_count):
    colatitude = math.pi * (jnp.arange(cycle_count, dtype=jnp.float32) + 0.5) / cycle_count
    cosines = jnp.cos(colatitude)[None, None, :]
    sine_values = jnp.sin(colatitude)
    order_real = order_index.astype(jnp.float32)
    steps_all = jnp.arange(1, degree_count + 1, dtype=jnp.float32)
    factors = jnp.log((2.0 * steps_all - 1.0) / (2.0 * steps_all))
    below_mask = (steps_all[None, :] <= order_real[:, None]).astype(jnp.float32)
    partial_log = jnp.sum(below_mask * factors[None, :], axis=1)
    start_log = 0.5 * jnp.log((2.0 * order_real + 1.0) / (4.0 * math.pi)) + 0.5 * partial_log
    start_log = start_log[:, None] + order_real[:, None] * jnp.log(sine_values)[None, :]
    order_col = order_real[None, :, None]
    block_count = degree_count // 16
    block_base = (16 * jnp.arange(block_count, dtype=jnp.int32)).astype(jnp.float32)[:, None, None]
    shape_all = (block_count, order_index.shape[0], cycle_count)
    unit_array = jnp.ones(shape_all, jnp.float32)
    zero_array = jnp.zeros(shape_all, jnp.float32)

    def product_half(half_turn, matrices):
        upper_left, upper_right, lower_left, lower_right, log_scale = matrices
        for inner_step in range(8):
            degree = block_base + (half_turn * 8 + inner_step).astype(jnp.float32)
            diag_top, off_top, off_low, diag_low = step_entries(degree, order_col, cosines)
            next_ul = diag_top * upper_left + off_top * lower_left
            next_ur = diag_top * upper_right + off_top * lower_right
            next_ll = off_low * upper_left + diag_low * lower_left
            next_lr = off_low * upper_right + diag_low * lower_right
            largest = jnp.maximum(
                jnp.maximum(jnp.abs(next_ul), jnp.abs(next_ur)),
                jnp.maximum(jnp.abs(next_ll), jnp.abs(next_lr)),
            )
            upper_left = next_ul / largest
            upper_right = next_ur / largest
            lower_left = next_ll / largest
            lower_right = next_lr / largest
            log_scale = log_scale + jnp.log(largest)
        return (upper_left, upper_right, lower_left, lower_right, log_scale)

    products = lax.fori_loop(
        0, 2, product_half, (unit_array, zero_array, zero_array, unit_array, zero_array)
    )

    def carry_block(vector_state, block_matrix):
        lead_value, lag_value, log_value = vector_state
        upper_left, upper_right, lower_left, lower_right, log_scale = block_matrix
        next_lead = upper_left * lead_value + upper_right * lag_value
        next_lag = lower_left * lead_value + lower_right * lag_value
        largest = jnp.maximum(jnp.abs(next_lead), jnp.abs(next_lag))
        return (
            (next_lead / largest, next_lag / largest, log_value + log_scale + jnp.log(largest)),
            vector_state,
        )

    initial = (unit_array[0], zero_array[0], start_log)
    final_state, starts = lax.scan(carry_block, initial, products)

    def degree_half(vector_state, half_turn):
        lead_value, lag_value, log_value = vector_state
        values = []
        for inner_step in range(8):
            degree = block_base + (half_turn * 8 + inner_step).astype(jnp.float32)
            diag_top, off_top, off_low, diag_low = step_entries(degree, order_col, cosines)
            next_lead = diag_top * lead_value + off_top * lag_value
            next_lag = off_low * lead_value + diag_low * lag_value
            largest = jnp.maximum(jnp.abs(next_lead), jnp.abs(next_lag))
            lead_value = next_lead / largest
            lag_value = next_lag / largest
            log_value = log_value + jnp.log(largest)
            values.append(lead_value * jnp.exp(log_value))
        return ((lead_value, lag_value, log_value), jnp.stack(values))

    last_state, table_rows = lax.scan(degree_half, starts, jnp.arange(2, dtype=jnp.int32))
    legendre = jnp.transpose(table_rows, (3, 2, 0, 1, 4)).reshape(
        order_index.shape[0], degree_count, cycle_count
    )
    degrees = jnp.arange(degree_count, dtype=jnp.int32)
    return jnp.where(degrees[None, :, None] >= order_index[:, None, None], legendre, 0.0)


def layer_norm(values, gain_row):
    values = values.astype(jnp.float32)
    average = jnp.mean(values, axis=-2, keepdims=True)
    centred = values - average
    variance = jnp.mean(centred * centred, axis=-2, keepdims=True)
    return centred * lax.rsqrt(variance + EPSILON) * gain_row.astype(jnp.float32)[:, None]


def mixing_matrix(weight):
    width = weight.shape[1]
    real_weight = weight[:, :, :width]
    imag_weight = weight[:, :, width:]
    top_half = jnp.concatenate([real_weight, imag_weight], axis=2)
    bottom_half = jnp.concatenate([-imag_weight, real_weight], axis=2)
    return jnp.concatenate([top_half, bottom_half], axis=1)


def order_list(sp_count, modes_dev):
    slots = jnp.arange(MMAX, dtype=jnp.int32)
    owner = slots // modes_dev
    within = slots % modes_dev
    mirrored = jnp.where(within % 2 == 0, owner, sp_count - 1 - owner)
    return within * sp_count + mirrored


def shards(field_in, spectral_gain, spectral_weight, mixer_gain, up_weight, up_bias, down_weight):
    grid_values = field_in[0]
    cycle_rows = grid_values.shape[0]
    sp_count = lax.axis_size("sp")
    device_rank = lax.axis_index("sp")
    modes_dev = MMAX // sp_count
    all_orders = order_list(sp_count, modes_dev)
    order_index = lax.dynamic_slice_in_dim(all_orders, device_rank * modes_dev, modes_dev, 0)
    cycle_index = device_rank * cycle_rows + jnp.arange(cycle_rows, dtype=jnp.int32)
    legendre = legendre_rows(order_index, NLAT, LMAX).astype(jnp.bfloat16)
    forward, inverse = fourier_tables(NLON, all_orders)
    weighting = quad_weights(cycle_index, NLAT) * (2.0 * math.pi / NLON)
    normed = layer_norm(grid_values, spectral_gain[0]).astype(jnp.bfloat16)
    spectral = jnp.einsum("nrm,acn->marc", forward, normed, preferred_element_type=jnp.float32)
    spectral = (
        (spectral * weighting[None, :, None, None])
        .astype(jnp.bfloat16)
        .reshape(MMAX, cycle_rows, 2 * C)
    )
    coeffs = jnp.einsum(
        "mla,mak->mlk",
        legendre,
        lax.all_to_all(spectral, "sp", split_axis=0, concat_axis=1, tiled=True),
        preferred_element_type=jnp.float32,
    ).astype(jnp.bfloat16)
    by_degree = lax.all_to_all(coeffs, "sp", split_axis=1, concat_axis=0, tiled=True)
    block_weight = mixing_matrix(spectral_weight[0])
    mixed_coeffs = jnp.einsum(
        "mlk,lkj->mlj", by_degree, block_weight, preferred_element_type=jnp.float32
    ).astype(jnp.bfloat16)
    grid_part = jnp.einsum(
        "mla,mlk->mak",
        legendre,
        lax.all_to_all(mixed_coeffs, "sp", split_axis=0, concat_axis=1, tiled=True),
        preferred_element_type=jnp.float32,
    ).astype(jnp.bfloat16)
    on_grid = lax.all_to_all(grid_part, "sp", split_axis=1, concat_axis=0, tiled=True)
    synthesis = jnp.einsum(
        "marc,rmn->acn",
        on_grid.reshape(MMAX, cycle_rows, 2, C),
        inverse,
        preferred_element_type=jnp.float32,
    )
    residual = grid_values.astype(jnp.float32) + synthesis
    hidden_in = layer_norm(residual, mixer_gain[0]).astype(jnp.bfloat16)
    hidden = jnp.einsum(
        "acn,ch->anh", hidden_in, up_weight[0], preferred_element_type=jnp.float32
    ) + up_bias[0].astype(jnp.float32)
    hidden = jax.nn.gelu(hidden, approximate=False).astype(jnp.bfloat16)
    branch = jnp.einsum("anh,ch->acn", hidden, down_weight[0], preferred_element_type=jnp.float32)
    result = (residual + branch).astype(jnp.bfloat16)
    received = passed_along(result, "section", 1)
    return received[None]


def solution(mesh):
    in_specs = (
        P("section", "sp", None, None),
        P("section", None),
        P("section", "sp", None, None),
        P("section", None),
        P("section", None, None),
        P("section", None),
        P("section", None, None),
    )
    out_specs = P("section", "sp", None, None)
    return jax.shard_map(shards, mesh=mesh, in_specs=in_specs, out_specs=out_specs, check_vma=False)
```

profile of v0, /device:TPU:4, one launch (start us, length us, event | category | flops | bytes accessed | tf_op | source)
XLA Modules:
  0.0 669.2 jit_solution(4990772788944840612)
XLA Ops:
  3.7 3.0 fusion.193
  6.7 5.1 cosine_convert_fusion
  11.8 4.7 multiply_convert_fusion.1
  16.5 7.0 %copy.42 = bf16[384,12,384]{2,1,0:T(8,128)(2,1)} copy(bf16[384,12,384]{0,2,1:T(8,128)(2,1)} %bitcast.453) | data formatting | bytes 7077888 | tf_op jit(solution)/shard_map/reshape | solution.py:192
  23.5 11.6 %all-to-all-start = ((bf16[384,12,384]{2,1,0:T(8,128)(2,1)}), bf16[384,12,384]{2,1,0:T(8,128)(2,1)}, u32[]{:S(2)}, u32[]{:S(2)}) async-start(bf16[384,12,384]{2,1,0:T(8,128)(2,1)} %copy.42), calls=%async_computation | async-start | bytes 9437184 | tf_op jit(solution)/shard_map/all_to_all | solution.py:197
  35.6 18.8 %while.70 = (s32[]{:T(128)}, f32[24,12,384]{2,1,0:T(8,128)S(1)}, f32[24,12,384]{2,1,0:T(8,128)S(1)}, f32[24,12,384]{2,1,0:T(8,128)S(1)}, f32[24,12,384]{2,1,0:T(...) while((s32[]{:T(128)}, f32[24,12,384]{2,1,0:T(8,128)S(1)}, ...), condition=%wide.region_2.3_spmd.clone.clone, body=%wide.region_1.2_spmd.clone.clone.sunk | while | flops 30785132 | bytes 43037432 | solution.py:109
  54.4 48.5 %while.69 = (s32[]{:T(128)}, f32[12,384]{1,0:T(8,128)S(1)}, f32[12,384]{1,0:T(8,128)S(1)}, f32[12,384]{1,0:T(8,128)S(1)}, f32[24,12,384]{2,1,0:T(8,128)}, /*inde...) while((s32[]{:T(128)}, f32[12,384]{1,0:T(8,128)S(1)}, ...), condition=%wide.region_4.5_spmd.clone, body=%wide.region_3.4_spmd.clone.sunk | while | flops 92163 | bytes 417957 | solution.py:125
  103.0 40.8 %while.68 = (s32[]{:T(128)}, f32[24,12,384]{2,1,0:T(8,128)}, f32[24,12,384]{2,1,0:T(8,128)}, f32[24,12,384]{2,1,0:T(8,128)S(1)}, bf16[2,8,24,12,384]{4,1,0,2,3:T...) while((s32[]{:T(128)}, f32[24,12,384]{2,1,0:T(8,128)}, ...), condition=%wide.region_6.7_spmd.clone.clone, body=%wide.region_5.6_spmd.clone.clone.sunk | while | flops 25144936 | bytes 60961436 | solution.py:142
  143.9 3.9 fusion.196
  147.8 5.2 copy.44
  153.0 7.1 %all_to_all.53 = bf16[12,384,384]{2,1,0:T(8,128)(2,1)} reshape(bf16[12,32,12,384]{3,2,1,0:T(8,128)(2,1)} %copy.44) | data formatting | bytes 7077888 | tf_op jit(solution)/shard_map/all_to_all | solution.py:197
  160.1 5.4 convolution_convert_fusion.1
  165.5 4.4 copy.45
  169.9 9.8 %all-to-all-start.1 = ((bf16[12,384,384]{2,0,1:T(8,128)(2,1)}), bf16[12,384,384]{2,0,1:T(8,128)(2,1)}, u32[]{:S(2)}, u32[]{:S(2)}) async-start(bf16[12,384,384]{2,0,1:T(8,128)(2,1)} %copy.45), calls=%async_computation.1 | async-start | bytes 9437184 | tf_op jit(solution)/shard_map/all_to_all | solution.py:200
  184.0 103.2 %all-to-all-done.1 = bf16[12,384,384]{2,0,1:T(8,128)(2,1)} async-done(((bf16[12,384,384]{2,0,1:T(8,128)(2,1)}), bf16[12,384,384]{2,0,1:T(8,128)(2,1)}, u32[]{:S(2)}, u32[]{:S(2)}) %all-to-all-start.1) | async-done | bytes 3538976 | tf_op jit(solution)/shard_map/all_to_all | solution.py:200
  287.2 5.2 copy.47
  292.4 6.8 %all_to_all.57 = bf16[384,12,384]{2,0,1:T(8,128)(2,1)} reshape(bf16[32,12,12,384]{3,1,0,2:T(8,128)(2,1)} %copy.47) | data formatting | bytes 7077888 | tf_op jit(solution)/shard_map/all_to_all | solution.py:200
  299.2 7.0 %convert_bitcast_fusion.1 = bf16[384,12,384]{0,2,1:T(8,128)(2,1)} fusion(bf16[384,12,384]{2,0,1:T(8,128)(2,1)} %all_to_all.57, bf16[12,192,192]{1,2,0:T(8,128)(2,1)} %get-tuple-element.1120, bf16[12,192,192]{1,2,0:T(8,128)(2,1)} %get-tuple-element.1119, bf16[12,192,384]{1,2,0:T(8,128)(2,1)S(1)} %bitcast.451), kind=kOutput, calls=%fused_computation.532 | convolution fusion | flops 1371340800 | bytes 10616832 | tf_op jit(solution)/shard_map/mlk,lkj->mlj/dot_general | solution.py:202
  306.2 7.0 %copy.48 = bf16[384,12,384]{2,1,0:T(8,128)(2,1)} copy(bf16[384,12,384]{0,2,1:T(8,128)(2,1)} %convert_bitcast_fusion.1) | data formatting | bytes 7077888 | tf_op jit(solution)/shard_map/convert_element_type | solution.py:204
  313.2 112.4 %all_to_all.69 = bf16[384,12,384]{2,1,0:T(8,128)(2,1)S(1)} all-to-all(bf16[384,12,384]{2,1,0:T(8,128)(2,1)} %copy.48), channel_id=1, replica_groups=mesh['section'=8,'sp'=32] {'sp'}, dimensions={0} | all-to-all | bytes 7077888 | tf_op jit(solution)/shard_map/all_to_all | solution.py:208
  428.4 6.8 %all_to_all.61 = bf16[12,384,384]{2,1,0:T(8,128)(2,1)} reshape(bf16[12,32,12,384]{3,2,1,0:T(8,128)(2,1)} %copy.50) | data formatting | bytes 7077888 | tf_op jit(solution)/shard_map/all_to_all | solution.py:208
  435.2 5.4 convolution_convert_fusion
  440.6 4.4 copy.52
  445.0 5.8 all-to-all-start.3
  451.0 5.5 multiply_convert_fusion.4
  456.5 102.4 %all-to-all-done.3 = bf16[12,384,384]{2,0,1:T(8,128)(2,1)} async-done(((bf16[12,384,384]{2,0,1:T(8,128)(2,1)}), bf16[12,384,384]{2,0,1:T(8,128)(2,1)}, u32[]{:S(2)}, u32[]{:S(2)}) %all-to-all-start.3) | async-done | bytes 3538976 | tf_op jit(solution)/shard_map/all_to_all | solution.py:211
  558.9 5.7 copy.54
  564.5 12.2 %reshape.7003 = bf16[384,12,2,192]{3,2,1,0:T(2,128)(2,1)} reshape(bf16[32,12,12,384]{3,2,1,0:T(8,128)(2,1)} %copy.54) | data formatting | bytes 7077888 | tf_op jit(solution)/shard_map/reshape | solution.py:214
  576.7 7.8 %fusion.319 = (f32[12,768]{1,0:T(8,128)S(1)}, f32[12,192,768]{2,1,0:T(8,128)S(1)}) fusion(bf16[1,384,768]{2,1,0:T(8,128)(2,1)S(1)} %get-tuple-element.1122, bf16[1,384,768]{2,1,0:T(8,128)(2,1)S(1)} %get-tuple-element.1121, bf16[384,12,2,192]{3,2,1,0:T(2,128)(2,1)} %reshape.7003, bf16[1,12,192,768]{3,2,1,0:T(8,128)(2,1)} %param.13), kind=kOutput, calls=%fused_computation.648 | convolution fusion | flops 2723798016 | bytes 15372288 | tf_op jit(solution)/shard_map/marc,rmn->acn/dot_general | solution.py:212
  585.4 6.5 fusion.199
  591.9 34.1 %fusion.197 = bf16[12,192,768]{2,1,0:T(8,128)(2,1)S(1)} fusion(f32[12,192,768]{2,1,0:T(8,128)S(1)} %get-tuple-element.1128, f32[12,768,384]{2,1,0:T(8,128)S(1)} %get-tuple-element.1129, f32[384]{0:T(512)S(1)} %convert_reduce_fusion.1, u16[768,384]{1,0:T(8,128)(2,1)S(1)} %get-tuple-element.775, u16[768,384]{1,0:T(8,128)(2,1)S(1)} %get-tuple-element.774, ...), kind=kOutput, calls=%fused_computation.509 | convolution fusion | flops 1613758464 | bytes 26101248 | tf_op jit(solution)/shard_map/anh,ch->acn/dot_general | solution.py:224
  626.1 40.9 %collective-permute-done = bf16[12,192,768]{2,1,0:T(8,128)(2,1)S(1)} collective-permute-done((bf16[12,192,768]{2,1,0:T(8,128)(2,1)S(1)}, bf16[12,192,768]{2,1,0:T(8,128)(2,1)S(1)}, u32[]{:S(2)}, u32[]{:S(2)}) %collective-permute-start) | collective-permute-done | bytes 3538976 | tf_op jit(solution)/shard_map/ppermute | solution.py:20
  (312 shorter events, 119.2 us)
Async XLA Ops:
  0.0 585.4 %copy-start = (bf16[1,192,384]{2,1,0:T(8,128)(2,1)S(1)}, bf16[1,192,384]{2,1,0:T(8,128)(2,1)}, u32[]{:S(2)}) copy-start(bf16[1,192,384]{2,1,0:T(8,128)(2,1)} %param.17) | copy-start | bytes 442372
  0.0 35.2 %copy-start.6 = (s32[384]{0:T(512)}, s32[384]{0:T(512)S(1)}, u32[]{:S(2)}) copy-start(s32[384]{0:T(512)S(1)} %fusion.258) | copy-start | bytes 4612
  0.1 11.8 %copy-start.3 = (bf16[1,12,192,768]{3,2,1,0:T(8,128)(2,1)S(1)}, bf16[1,12,192,768]{3,2,1,0:T(8,128)(2,1)}, u32[]{:S(2)}) copy-start(bf16[1,12,192,768]{3,2,1,0:T(8,128)(2,1)} %param.13) | copy-start | bytes 10616836
  23.5 124.3 %all-to-all-start = ((bf16[384,12,384]{2,1,0:T(8,128)(2,1)}), bf16[384,12,384]{2,1,0:T(8,128)(2,1)}, u32[]{:S(2)}, u32[]{:S(2)}) async-start(bf16[384,12,384]{2,1,0:T(8,128)(2,1)} %copy.42), calls=%async_computation | async-start | bytes 9437184 | tf_op jit(solution)/shard_map/all_to_all | solution.py:197
  39.3 3.2 copy-start.1
  44.1 0.8 copy-start.2
  48.7 3.2 copy-start.1
  53.5 0.8 copy-start.2
  112.1 8.4 %copy-start.4 = (bf16[2,8,24,12,384]{4,1,0,2,3:T(8,128)(2,1)S(1)}, bf16[2,8,24,12,384]{4,1,0,2,3:T(8,128)(2,1)}, u32[]{:S(2)}) copy-start(bf16[2,8,24,12,384]{4,1,0,2,3:T(8,128)(2,1)} %get-tuple-element.1879) | copy-start | bytes 10616836 | tf_op jit(solution)/shard_map/while
  121.7 1.8 copy-start.5
  132.4 8.4 %copy-start.4 = (bf16[2,8,24,12,384]{4,1,0,2,3:T(8,128)(2,1)S(1)}, bf16[2,8,24,12,384]{4,1,0,2,3:T(8,128)(2,1)}, u32[]{:S(2)}) copy-start(bf16[2,8,24,12,384]{4,1,0,2,3:T(8,128)(2,1)} %get-tuple-element.1879) | copy-start | bytes 10616836 | tf_op jit(solution)/shard_map/while
  142.0 1.8 copy-start.5
  169.9 117.3 %all-to-all-start.1 = ((bf16[12,384,384]{2,0,1:T(8,128)(2,1)}), bf16[12,384,384]{2,0,1:T(8,128)(2,1)}, u32[]{:S(2)}, u32[]{:S(2)}) async-start(bf16[12,384,384]{2,0,1:T(8,128)(2,1)} %copy.45), calls=%async_computation.1 | async-start | bytes 9437184 | tf_op jit(solution)/shard_map/all_to_all | solution.py:200
  440.6 10.3 %copy-start.9 = (bf16[1,192]{1,0:T(2,128)(2,1)S(1)}, bf16[1,192]{1,0:T(2,128)(2,1)}, u32[]{:S(2)}) copy-start(bf16[1,192]{1,0:T(2,128)(2,1)} %param.16) | copy-start | bytes 1156
  440.6 10.3 %copy-start.8 = (bf16[1,384]{1,0:T(2,128)(2,1)S(1)}, bf16[1,384]{1,0:T(2,128)(2,1)}, u32[]{:S(2)}) copy-start(bf16[1,384]{1,0:T(2,128)(2,1)} %param.18) | copy-start | bytes 2308
  440.6 10.4 %copy-start.7 = (s32[384]{0:T(512)S(1)}, s32[384]{0:T(512)}, u32[]{:S(2)}) copy-start(s32[384]{0:T(512)} %copy-done.6) | copy-start | bytes 4612
  445.0 113.8 %all-to-all-start.3 = ((bf16[12,384,384]{2,0,1:T(8,128)(2,1)}), bf16[12,384,384]{2,0,1:T(8,128)(2,1)}, u32[]{:S(2)}, u32[]{:S(2)}) async-start(bf16[12,384,384]{2,0,1:T(8,128)(2,1)} %copy.52), calls=%async_computation.3 | async-start | bytes 9437184 | tf_op jit(solution)/shard_map/all_to_all | solution.py:211
  585.4 6.6 copy-start.10
  626.1 40.9 %collective-permute-start = (bf16[12,192,768]{2,1,0:T(8,128)(2,1)S(1)}, bf16[12,192,768]{2,1,0:T(8,128)(2,1)S(1)}, u32[]{:S(2)}, u32[]{:S(2)}) collective-permute-start(bf16[12,192,768]{2,1,0:T(8,128)(2,1)S(1)} %fusion.197), channel_id=1, source_target_pairs={{0,32},{32,64},{64,96},{96,128},{128,160},{160,192},{192,224},{224... | collective-permute-start | bytes 10616840 | tf_op jit(solution)/shard_map/ppermute | solution.py:20
where the time goes:
time: 680 us; the launch traced here: 669 us
  waiting for transfers between devices  246 us (36%)
  other arithmetic  122 us (18%)
  blocking collectives  112 us (16%)
  local copies, waits for them, and re-layouts  86.8 us (13%)
  matrix products  71 us (10%)
  starting transfers between devices  27.3 us (4%)
    all_to_all x1, blocking collectives, shards(): lax.all_to_all(mixed_coeffs, 'sp', split_axis=0, concat_axis=1, tiled=True)  112 us
    all_to_all x1, waiting for transfers between devices, shards(): lax.all_to_all(coeffs, 'sp', split_axis=1, concat_axis=0, tiled=True)  103 us
    all_to_all x1, waiting for transfers between devices, shards(): lax.all_to_all(grid_part, 'sp', split_axis=1, concat_axis=0, tiled=True)  102 us
    ppermute x1, waiting for transfers between devices, passed_along(): lax.ppermute(value, axis, [(i, (i + by) % count) for i in range(count)])  40.9 us
    dot_general x1, matrix products, shards(): jnp.einsum('anh,ch->acn', hidden, down_weight[0], preferred_element_type=...  34.1 us
    dynamic_update_slice x48, other arithmetic, legendre_rows(): final_state, starts = lax.scan(carry_block, initial, products)  29.2 us
    while x14, other arithmetic  24.6 us
    add x24, other arithmetic, carry_block(): log_value + log_scale + jnp.log(largest)  18.4 us
  transfers between devices with their start and end apart: 4, of which 3 were waited for; matrix products, arithmetic and copies ran while one was open for 17% of the time, Pallas kernels for 0%

commit v1 on v0

v1 whole, which is shorter than its diff:
```python
import math

import jax
import jax.numpy as jnp
from jax import lax
from jax.experimental import pallas as pl
from jax.experimental.pallas import tpu as pltpu
from jax.sharding import PartitionSpec as P


C = 192
HID = 384
NLAT = 384
NLON = 768
LMAX = 384
MMAX = 384
SP = 32
ROWS = NLAT // SP
PAIRS = LMAX // SP // 2
K2 = 2 * C
BLOCK_M = 2 * PAIRS * ROWS
BLOCK_L = 2 * PAIRS * PAIRS
T_ROWS = LMAX
T_PAD = T_ROWS + 8
LANES = 2 * NLAT

EPSILON = 1e-05
SCALE_LOG2 = 64.0
DOWN = 2.0**-64
LIMIT = 2.0**32

F32 = jnp.float32
BF16 = jnp.bfloat16


def pair_low(pair):
    return jnp.minimum(2 * pair, LMAX - 1 - 2 * pair)


def pair_high(pair):
    return jnp.maximum(2 * pair, LMAX - 1 - 2 * pair)


def params(mebibytes):
    return pltpu.CompilerParams(vmem_limit_bytes=mebibytes * 1024 * 1024)


def whole(shape):
    return pl.BlockSpec(shape, lambda *_: (0,) * len(shape))


def quad_weights(cycle_index, cycle_count):
    terms_count = cycle_count // 2
    orders = jnp.arange(1, terms_count + 1, dtype=jnp.int32)
    phase_turns = orders[None, :] * (2 * cycle_index[:, None] + 1) % (2 * cycle_count)
    angles = math.pi * phase_turns.astype(F32) / cycle_count
    orders_real = orders.astype(F32)
    series = jnp.sum(jnp.cos(angles) / (4.0 * orders_real * orders_real - 1.0)[None, :], axis=1)
    return 2.0 / cycle_count * (1.0 - 2.0 * series)


def norm_rows(values, gain):
    average = jnp.mean(values, axis=0, keepdims=True)
    centred = values - average
    variance = jnp.mean(centred * centred, axis=0, keepdims=True)
    return centred * lax.rsqrt(variance + EPSILON) * gain


def analysis_kernel(
    weight_ref, field_ref, gain_ref, cosb_ref, sinb_ref, cosa_ref, sina_ref, out_ref, table_ref, normed_ref, acc_ref
):
    step = pl.program_id(0)

    @pl.when(step == 0)
    def _():
        normed_ref[0:64] = jnp.zeros((64, NLON), BF16)
        normed_ref[256:320] = jnp.zeros((64, NLON), BF16)
        cosb, sinb = cosb_ref[...], sinb_ref[...]
        for part in range(NLON // 128):
            cosa, sina = cosa_ref[:, part : part + 1], sina_ref[:, part : part + 1]
            lanes = slice(128 * part, 128 * part + 128)
            table_ref[0, :, lanes] = (cosa * cosb - sina * sinb).astype(BF16)
            table_ref[1, :, lanes] = (-(sina * cosb + cosa * sinb)).astype(BF16)

    normed_ref[64:256] = norm_rows(field_ref[...].astype(F32), gain_ref[...]).astype(BF16)
    dims = (((1,), (1,)), ((), ()))
    real = lax.dot_general(table_ref[0], normed_ref[64:320], dims, preferred_element_type=F32)
    imag = lax.dot_general(table_ref[1], normed_ref[0:256], dims, preferred_element_type=F32)
    weight = weight_ref[step]
    rows = pl.ds(step, MMAX, stride=ROWS)
    acc_ref[0, rows, :] = real[:, 0:128] * weight
    acc_ref[1, rows, :] = (real[:, 128:256] + imag[:, 0:128]) * weight
    acc_ref[2, rows, :] = imag[:, 128:256] * weight

    @pl.when(step == ROWS - 1)
    def _():
        @pl.loop(0, MMAX * ROWS // 256)
        def _(piece):
            rows = pl.ds(pl.multiple_of(piece * 256, 256), 256)
            for part in range(3):
                out_ref[rows, 128 * part : 128 * part + 128] = acc_ref[part, rows, :].astype(BF16)


def analysis(field, gain, weighting, cosb, sinb, cosa, sina):
    return pl.pallas_call(
        analysis_kernel,
        grid=(ROWS,),
        in_specs=[
            pl.BlockSpec(memory_space=pltpu.SMEM),
            pl.BlockSpec((None, C, NLON), lambda j: (j, 0, 0)),
            whole((C, 1)),
            whole((MMAX, 128)),
            whole((MMAX, 128)),
            whole((MMAX, 8)),
            whole((MMAX, 8)),
        ],
        out_specs=[whole((MMAX * ROWS, K2)), whole((2, MMAX, NLON))],
        out_shape=[
            jax.ShapeDtypeStruct((MMAX * ROWS, K2), BF16),
            jax.ShapeDtypeStruct((2, MMAX, NLON), BF16),
        ],
        scratch_shapes=[pltpu.VMEM((320, NLON), BF16), pltpu.VMEM((3, MMAX * ROWS, 128), F32)],
        compiler_params=params(26),
        cost_estimate=pl.CostEstimate(flops=3_600_000_000, bytes_accessed=9_000_000, transcendentals=0),
        name="analysis",
    )(weighting, field, gain, cosb, sinb, cosa, sina)


def legendre_kernel(orders_ref, cosine_ref, low_ref, start_ref, out_ref, acc_ref, diag_ref):
    step = pl.program_id(0)

    @pl.when(step == 0)
    def _():
        order = [orders_ref[0], orders_ref[1]]
        order_sq = [order[0] * order[0], order[1] * order[1]]
        cosine = cosine_ref[...]
        is_low = low_ref[...] > 0.5
        start = start_ref[...]
        start_level = jnp.floor(start * (1.0 / SCALE_LOG2) + 0.5)
        start_lead = jnp.exp2(start - SCALE_LOG2 * start_level)

        def spread(pair):
            return jnp.where(
                is_low,
                jnp.concatenate([pair[0]] * (LANES // 128), axis=1),
                jnp.concatenate([pair[1]] * (LANES // 128), axis=1),
            )

        order_lanes = spread(order)

        def advance(degree_index, state):
            lead, lag, level = state
            degree = degree_index.astype(F32)
            degree_sq = degree * degree
            degree_norm = jnp.maximum(4.0 * degree_sq - 1.0, 0.0)
            before_sq = (degree - 1.0) * (degree - 1.0)
            before_norm = jnp.maximum(4.0 * before_sq - 1.0, 1.0)
            leading, trailing = [], []
            for one_sq in order_sq:
                lead_coeff = jnp.sqrt(degree_norm / jnp.maximum(degree_sq - one_sq, 1.0))
                leading.append(lead_coeff)
                trailing.append(lead_coeff * jnp.sqrt(jnp.maximum(before_sq - one_sq, 0.0) / before_norm))
            following = spread(leading) * cosine * lead - spread(trailing) * lag
            first = order_lanes == degree
            lag = jnp.where(first, 0.0, lead)
            lead = jnp.where(first, start_lead, following)
            level = jnp.where(first, start_level, level)
            large = jnp.abs(lead) > LIMIT
            lead = jnp.where(large, lead * DOWN, lead)
            lag = jnp.where(large, lag * DOWN, lag)
            level = jnp.where(large, level + 1.0, level)
            value = lead * jnp.where(level > -0.5, 1.0, DOWN)
            value = value * jnp.where(level > -1.5, 1.0, jnp.where(level > -2.5, DOWN, 0.0))
            return (lead, lag, level), value, first

        def position(degree_index):
            odd = lax.rem(degree_index, 2)
            pair = jnp.where(odd == 0, degree_index, LMAX - 1 - degree_index) // 2
            return pl.multiple_of(pair * 16, 16)

        def lower(degree_index, state):
            state, value, _ = advance(degree_index, state)
            rows = pl.ds(position(degree_index) + 8, 8)
            low = jnp.where(is_low, value, 0.0)
            for part in range(LANES // 128):
                acc_ref[part, rows, :] = low[:, 128 * part : 128 * part + 128]
            return state

        def upper(degree_index, state):
            state, value, first = advance(degree_index, state)
            base = position(degree_index)
            low = jnp.where(is_low, value, 0.0)
            high = jnp.where(is_low, 0.0, value)
            added = jnp.where(first, 0.0, high)
            for part in range(LANES // 128):
                lanes = slice(128 * part, 128 * part + 128)
                acc_ref[part, pl.ds(base, 8), :] = low[:, lanes]
                acc_ref[part, pl.ds(base + 8, 8), :] += added[:, lanes]
            diag_ref[...] += jnp.where(first, high, 0.0)
            return state

        diag_ref[...] = jnp.zeros_like(diag_ref)
        zero = jnp.zeros((8, LANES), F32)
        state = lax.fori_loop(0, LMAX // 2, lower, (zero, zero, zero))
        lax.fori_loop(LMAX // 2, LMAX, upper, state)

    for part in range(LANES // 128):
        rows = acc_ref[part, pl.ds(step, T_ROWS, stride=8), :]
        out_ref[0:T_ROWS, 128 * part : 128 * part + 128] = rows.astype(BF16)
    row = lax.broadcasted_iota(jnp.int32, (8, LANES), 0)
    out_ref[T_ROWS:T_PAD] = jnp.where(row == 0, diag_ref[pl.ds(step, 1), :], 0.0).astype(BF16)


def legendre_table(orders, cosine, low, start):
    return pl.pallas_call(
        legendre_kernel,
        grid=(PAIRS,),
        in_specs=[whole((2, 8, 128)), whole((8, LANES)), whole((8, LANES)), whole((8, LANES))],
        out_specs=pl.BlockSpec((None, T_PAD, LANES), lambda i: (i, 0, 0)),
        out_shape=jax.ShapeDtypeStruct((PAIRS, T_PAD, LANES), BF16),
        scratch_shapes=[pltpu.VMEM((LANES // 128, T_ROWS * 8, 128), F32), pltpu.VMEM((8, LANES), F32)],
        compiler_params=params(22),
        cost_estimate=pl.CostEstimate(flops=10_000_000_000, bytes_accessed=4_000_000, transcendentals=0),
        name="legendre_table",
    )(orders, cosine, low, start)


def forward_kernel(table_ref, spectral_ref, out_ref, diag_ref, acc_ref):
    step = pl.program_id(0)
    values = spectral_ref[...].reshape(LANES, K2)
    result = jnp.dot(table_ref[...], values, preferred_element_type=F32)
    for part in range(3):
        acc_ref[part, pl.ds(step, T_ROWS, stride=PAIRS), :] = result[0:T_ROWS, 128 * part : 128 * part + 128]
    row = lax.broadcasted_iota(jnp.int32, (8, K2), 0)

    @pl.when(step == 0)
    def _():
        diag_ref[...] = jnp.zeros_like(diag_ref)

    diag_ref[...] = jnp.where(row == step, result[T_ROWS : T_ROWS + 1], diag_ref[...])

    @pl.when(step == PAIRS - 1)
    def _():
        @pl.loop(0, SP * BLOCK_L // 256)
        def _(piece):
            rows = pl.ds(pl.multiple_of(piece * 256, 256), 256)
            for part in range(3):
                out_ref[rows, 128 * part : 128 * part + 128] = acc_ref[part, rows, :].astype(BF16)


def forward(table, spectral):
    return pl.pallas_call(
        forward_kernel,
        grid=(PAIRS,),
        in_specs=[
            pl.BlockSpec((None, T_PAD, LANES), lambda i: (i, 0, 0)),
            pl.BlockSpec((SP, None, 2 * ROWS, K2), lambda i: (0, i, 0, 0)),
        ],
        out_specs=[whole((SP * BLOCK_L, K2)), whole((8, K2))],
        out_shape=[jax.ShapeDtypeStruct((SP * BLOCK_L, K2), BF16), jax.ShapeDtypeStruct((8, K2), F32)],
        scratch_shapes=[pltpu.VMEM((3, SP * BLOCK_L, 128), F32)],
        compiler_params=params(16),
        cost_estimate=pl.CostEstimate(flops=1_400_000_000, bytes_accessed=9_000_000, transcendentals=0),
        name="forward",
    )(table, spectral)


def mixing_kernel(rank_ref, coeffs_ref, own_ref, other_ref, diag_ref, out_ref, diag_out_ref):
    step = pl.program_id(0)
    rank = rank_ref[0]
    own_is_low = rank < SP // 2
    values = coeffs_ref[...].reshape(SP * 24, K2)
    index = lax.broadcasted_iota(jnp.int32, (SP * 24, 1), 0)
    owner = index // 24
    within = index - owner * 24
    local = within // 12
    within = within - local * 12
    second = within // 6
    order = pair_low(owner * PAIRS + within - second * 6)
    low_degree = pair_low(rank * PAIRS + 2 * step + local)
    uses_low = jnp.logical_and(second == 1, order <= low_degree)
    uses_own = uses_low == own_is_low
    result = []
    for pair in range(2):
        own = jnp.dot(values, own_ref[pair], preferred_element_type=F32)
        other = jnp.dot(values, other_ref[pair], preferred_element_type=F32)
        result.append(jnp.where(uses_own, own, other))
    mixed = jnp.where(local == 0, result[0], result[1]).astype(BF16)
    out_ref[...] = mixed.reshape(SP, 24, K2)

    @pl.when(step == 0)
    def _():
        diag_out_ref[...] = jnp.zeros_like(diag_out_ref)

    diag = diag_ref[...].astype(BF16)
    row = lax.broadcasted_iota(jnp.int32, (8, K2), 0)
    for pair in range(2):
        own = jnp.dot(diag, own_ref[pair], preferred_element_type=F32)
        other = jnp.dot(diag, other_ref[pair], preferred_element_type=F32)
        chosen = jnp.where(own_is_low, other, own)
        diag_out_ref[...] = jnp.where(row == 2 * step + pair, chosen, diag_out_ref[...])


def mixing(rank, coeffs, own, other, diag):
    block = pl.BlockSpec((SP, 24, K2), lambda g: (0, g, 0))
    weight = pl.BlockSpec((2, K2, K2), lambda g: (g, 0, 0))
    return pl.pallas_call(
        mixing_kernel,
        grid=(PAIRS // 2,),
        in_specs=[pl.BlockSpec(memory_space=pltpu.SMEM), block, weight, weight, whole((8, K2))],
        out_specs=[block, whole((8, K2))],
        out_shape=[jax.ShapeDtypeStruct((SP, BLOCK_L, K2), BF16), jax.ShapeDtypeStruct((8, K2), F32)],
        compiler_params=params(20),
        cost_estimate=pl.CostEstimate(flops=2_700_000_000, bytes_accessed=7_000_000, transcendentals=0),
        name="mixing",
    )(rank, coeffs, own, other, diag)


def inverse_kernel(table_ref, mixed_ref, diag_ref, out_ref, acc_ref):
    step = pl.program_id(0)

    @pl.when(step == 0)
    def _():
        @pl.loop(0, SP * BLOCK_L // 256)
        def _(piece):
            rows = pl.ds(pl.multiple_of(piece * 256, 256), 256)
            for part in range(3):
                acc_ref[part, rows, :] = mixed_ref[rows, 128 * part : 128 * part + 128].astype(F32)

    rows = pl.ds(step, T_ROWS, stride=PAIRS)
    values = jnp.concatenate([acc_ref[part, rows, :] for part in range(3)], axis=1).astype(BF16)
    row = lax.broadcasted_iota(jnp.int32, (8, K2), 0)
    diag = jnp.where(row == 0, diag_ref[pl.ds(step, 1), :], 0.0).astype(BF16)
    dims = (((0,), (0,)), ((), ()))
    result = lax.dot_general(table_ref[0:T_ROWS], values, dims, preferred_element_type=F32)
    result += lax.dot_general(table_ref[T_ROWS:T_PAD], diag, dims, preferred_element_type=F32)
    out_ref[...] = result.astype(BF16).reshape(SP, 2 * ROWS, K2)


def inverse(table, mixed, diag):
    return pl.pallas_call(
        inverse_kernel,
        grid=(PAIRS,),
        in_specs=[
            pl.BlockSpec((None, T_PAD, LANES), lambda i: (i, 0, 0)),
            whole((SP * BLOCK_L, K2)),
            whole((8, K2)),
        ],
        out_specs=pl.BlockSpec((SP, None, 2 * ROWS, K2), lambda i: (0, i, 0, 0)),
        out_shape=jax.ShapeDtypeStruct((SP, PAIRS, 2 * ROWS, K2), BF16),
        scratch_shapes=[pltpu.VMEM((3, SP * BLOCK_L, 128), F32)],
        compiler_params=params(18),
        cost_estimate=pl.CostEstimate(flops=1_400_000_000, bytes_accessed=9_000_000, transcendentals=0),
        name="inverse",
    )(table, mixed, diag)


def synthesis_kernel(
    grid_ref, field_ref, table_ref, gain_ref, up_ref, bias_ref, down_ref, out_ref, acc_ref
):
    step = pl.program_id(0)

    @pl.when(step == 0)
    def _():
        @pl.loop(0, MMAX * ROWS // 256)
        def _(piece):
            rows = pl.ds(pl.multiple_of(piece * 256, 256), 256)
            for part in range(3):
                acc_ref[part, rows, :] = grid_ref[rows, 128 * part : 128 * part + 128].astype(F32)

    rows = pl.ds(step, MMAX, stride=ROWS)
    values = jnp.concatenate([acc_ref[part, rows, :] for part in range(3)], axis=1)
    row = lax.broadcasted_iota(jnp.int32, (MMAX, K2), 0)
    values = jnp.where(row == 0, values, 2.0 * values)
    turned = values.T.astype(BF16)
    residual = field_ref[...].astype(F32)
    residual += jnp.dot(turned[0:C], table_ref[0], preferred_element_type=F32)
    residual += jnp.dot(turned[C:K2], table_ref[1], preferred_element_type=F32)
    hidden_in = norm_rows(residual, gain_ref[...]).astype(BF16)
    hidden = jnp.dot(up_ref[...], hidden_in, preferred_element_type=F32) + bias_ref[...]
    hidden = hidden * (1.0 + lax.erf(hidden * math.sqrt(0.5))) * 0.5
    branch = jnp.dot(down_ref[...], hidden.astype(BF16), preferred_element_type=F32)
    out_ref[...] = (residual + branch).astype(BF16)


def synthesis(on_grid, field, table, gain, up, bias, down):
    cycle = pl.BlockSpec((None, C, NLON), lambda j: (j, 0, 0))
    return pl.pallas_call(
        synthesis_kernel,
        grid=(ROWS,),
        in_specs=[
            whole((MMAX * ROWS, K2)),
            cycle,
            whole((2, MMAX, NLON)),
            whole((C, 1)),
            whole((HID, C)),
            whole((HID, 1)),
            whole((C, HID)),
        ],
        out_specs=cycle,
        out_shape=jax.ShapeDtypeStruct((ROWS, C, NLON), BF16),
        scratch_shapes=[pltpu.VMEM((3, MMAX * ROWS, 128), F32)],
        compiler_params=params(32),
        cost_estimate=pl.CostEstimate(flops=8_000_000_000, bytes_accessed=12_000_000, transcendentals=0),
        name="synthesis",
    )(on_grid, field, table, gain, up, bias, down)


def mixing_matrix(weight):
    real_weight = weight[:, :, :C]
    imag_weight = weight[:, :, C:]
    bottom_half = jnp.concatenate([-imag_weight, real_weight], axis=2)
    return jnp.concatenate([weight, bottom_half], axis=1)


def to_next(value):
    count = lax.axis_size("section")
    return lax.ppermute(value, "section", [(i, (i + 1) % count) for i in range(count)])


def to_mirrored(value):
    count = lax.axis_size("sp")
    return lax.ppermute(value, "sp", [(d, count - 1 - d) for d in range(count)])


def exchange(value):
    return lax.all_to_all(value, "sp", split_axis=0, concat_axis=0)


def legendre_inputs(rank):
    pair = rank * PAIRS + jnp.minimum(jnp.arange(8, dtype=jnp.int32), PAIRS - 1)
    orders = jnp.stack([pair_low(pair), pair_high(pair)]).astype(F32)
    lane = jnp.arange(LANES, dtype=jnp.int32)
    low = (lane // ROWS) % 2 == 0
    cycle = lane // (2 * ROWS) * ROWS + lane % ROWS
    colatitude = math.pi * (cycle.astype(F32) + 0.5) / NLAT
    steps_all = jnp.arange(1, LMAX + 1, dtype=F32)
    factors = jnp.log((2.0 * steps_all - 1.0) / (2.0 * steps_all))
    below = (steps_all <= orders[:, :, None]).astype(F32)
    partial_log = jnp.sum(below * factors, axis=2)
    start = 0.5 * jnp.log((2.0 * orders + 1.0) / (4.0 * math.pi)) + 0.5 * partial_log
    order_lanes = jnp.where(low, orders[0][:, None], orders[1][:, None])
    start = jnp.where(low, start[0][:, None], start[1][:, None])
    start = (start + order_lanes * jnp.log(jnp.sin(colatitude))) * (1.0 / math.log(2.0))
    return (
        jnp.broadcast_to(orders[:, :, None], (2, 8, 128)),
        jnp.broadcast_to(jnp.cos(colatitude), (8, LANES)),
        jnp.broadcast_to(low.astype(F32), (8, LANES)),
        start,
    )


def fourier_inputs():
    pair = jnp.arange(MMAX // 2, dtype=jnp.int32)
    orders = jnp.stack([pair_low(pair), pair_high(pair)], axis=1).reshape(MMAX, 1)
    fine = (2.0 * math.pi / NLON) * (orders * jnp.arange(128, dtype=jnp.int32) % NLON).astype(F32)
    coarse = (2.0 * math.pi / 6) * (orders * jnp.arange(8, dtype=jnp.int32) % 6).astype(F32)
    return (jnp.cos(fine), jnp.sin(fine), jnp.cos(coarse), jnp.sin(coarse))


def block(field_in, spectral_gain, spectral_weight, mixer_gain, up_weight, up_bias, down_weight):
    field = field_in[0]
    rank = lax.axis_index("sp")
    weighting = quad_weights(rank * ROWS + jnp.arange(ROWS, dtype=jnp.int32), NLAT) * (2.0 * math.pi / NLON)
    spectral, table = analysis(
        field, spectral_gain.reshape(C, 1).astype(F32), weighting, *fourier_inputs()
    )
    rank_after, weight, _ = lax.optimization_barrier((rank, spectral_weight[0], spectral))
    by_order = exchange(spectral.reshape(SP, BLOCK_M, K2))
    weight = to_next(weight)
    own_weight, other_weight = weight[0::2], weight[1::2][::-1]
    legendre = legendre_table(*legendre_inputs(rank_after))

    by_order, other_weight = lax.optimization_barrier((by_order, other_weight))
    other_weight = to_mirrored(other_weight)
    coeffs, diag = forward(legendre, by_order.reshape(SP, PAIRS, 2 * ROWS, K2))
    coeffs = to_next(coeffs)
    diag = to_next(diag)
    by_degree = exchange(coeffs.reshape(SP, BLOCK_L, K2))
    own_matrix, other_matrix = mixing_matrix(own_weight), mixing_matrix(other_weight)
    mixed, diag = mixing(rank.reshape(1), by_degree, own_matrix, other_matrix, diag)
    back = exchange(mixed)
    grid_part = inverse(legendre, back.reshape(SP * BLOCK_L, K2), diag)
    on_grid = exchange(grid_part.reshape(SP, BLOCK_M, K2))
    next_field = to_next(field)
    gain_next, bias_next = to_next(mixer_gain), to_next(up_bias)
    up_next, down_next = to_next(up_weight), to_next(down_weight)
    result = synthesis(
        on_grid.reshape(MMAX * ROWS, K2),
        next_field,
        table,
        gain_next.reshape(C, 1).astype(F32),
        up_next[0].T,
        bias_next.reshape(HID, 1).astype(F32),
        down_next[0],
    )
    return result[None]


def solution(mesh):
    in_specs = (
        P("section", "sp", None, None),
        P("section", None),
        P("section", "sp", None, None),
        P("section", None),
        P("section", None, None),
        P("section", None),
        P("section", None, None),
    )
    out_specs = P("section", "sp", None, None)
    return jax.shard_map(block, mesh=mesh, in_specs=in_specs, out_specs=out_specs, check_vma=False)
```

time: 680 us -> 401 us (0.59); the launches traced: 669 us -> 400 us
  other arithmetic: 122 us -> 5.46 us
  matrix products: 71 us -> 0 us
  Pallas kernels: 0 us -> 65.1 us
  blocking collectives: 112 us -> 48.5 us
  local copies, waits for them, and re-layouts: 86.8 us -> 23.5 us
  waiting for transfers between devices: 246 us -> 229 us
    all_to_all x3, waiting for transfers between devices: 206 us -> 92.8 us  [exchange(): return lax.all_to_all(value, 'sp', split_axis=0, concat_axis=0)]
    ppermute x1 -> x9, waiting for transfers between devices: 40.9 us -> 136 us  [the longest x1 74.2 us: to_mirrored(): return lax.ppermute(value, 'sp', [(d, count - 1 - d) for d in range(count)])]
    dot_general x7 -> x0, matrix products: 71 us -> none  [the longest x1 34.1 us: shards(): jnp.einsum('anh,ch->acn', hidden, down_weight[0], preferred_element_type=...]
    pallas_call x0 -> x6, Pallas kernels: none -> 65.1 us  [the longest x1 20.3 us: legendre_table(): pl.pallas_call(legendre_kernel, grid=(PAIRS,), in_specs=[whole((2, 8, 128...]
    all_to_all x1, blocking collectives: 112 us -> 48.5 us  [exchange(): return lax.all_to_all(value, 'sp', split_axis=0, concat_axis=0)]
    all_to_all x7 -> x0, local copies, waits for them, and re-layouts: 39.5 us -> none  [the longest x2 12.3 us: shards(): lax.all_to_all(spectral, 'sp', split_axis=0, concat_axis=1, tiled=True)]
    dynamic_update_slice x48 -> x0, other arithmetic: 29.2 us -> none  [legendre_rows(): final_state, starts = lax.scan(carry_block, initial, products)]
    while x14 -> x0, other arithmetic: 24.6 us -> none
  transfers between devices with their start and end apart: 4 -> 12, of which waited for: 3 -> 7; matrix products, arithmetic and copies ran while one was open for 17% -> 3% of each run, Pallas kernels for 0% -> 5%
where the time goes in v1:
time: 401 us; the launch traced here: 400 us
  waiting for transfers between devices  229 us (57%)
  Pallas kernels  65.1 us (16%)
  blocking collectives  48.5 us (12%)
  starting transfers between devices  28.2 us (7%)
  local copies, waits for them, and re-layouts  23.5 us (6%)
  other arithmetic  5.46 us (1%)
    all_to_all x3, waiting for transfers between devices, exchange(): return lax.all_to_all(value, 'sp', split_axis=0, concat_axis=0)  92.8 us
    ppermute x1, waiting for transfers between devices, to_mirrored(): return lax.ppermute(value, 'sp', [(d, count - 1 - d) for d in range(count)])  74.2 us
    ppermute x8, waiting for transfers between devices, to_next(): lax.ppermute(value, 'section', [(i, (i + 1) % count) for i in range(count)])  61.9 us
    all_to_all x1, blocking collectives, exchange(): return lax.all_to_all(value, 'sp', split_axis=0, concat_axis=0)  48.5 us
    all_to_all x3, starting transfers between devices, exchange(): return lax.all_to_all(value, 'sp', split_axis=0, concat_axis=0)  21.1 us
    pallas_call x1, Pallas kernels, legendre_table(): pl.pallas_call(legendre_kernel, grid=(PAIRS,), in_specs=[whole((2, 8, 128...  20.3 us
    pallas_call x1, Pallas kernels, synthesis(): pl.pallas_call(synthesis_kernel, grid=(ROWS,), in_specs=[whole((MMAX * RO...  17.2 us
    unnamed x33, local copies, waits for them, and re-layouts  16.2 us
  transfers between devices with their start and end apart: 12, of which 7 were waited for; matrix products, arithmetic and copies ran while one was open for 3% of the time, Pallas kernels for 5%

profile of v1, /device:TPU:4, one launch (start us, length us, event | category | flops | bytes accessed | tf_op | source)
XLA Modules:
  0.0 400.0 jit_solution(9278649578197343579)
XLA Ops:
  0.3 0.9 fusion.4
  3.2 2.0 copy-done.7
  5.2 10.6 %analysis.1 = (bf16[4608,384]{1,0:T(8,128)(2,1)S(1)}, bf16[2,384,768]{2,1,0:T(8,128)(2,1)S(1)}) custom-call(f32[12]{0:T(128)S(1)} %subtract_multiply_fusion.weight_ref, bf16[12,192,768]{2,1,0:T(8,128)(2,1)S(1)} %bitcast.36, f32[192,1]{1,0:T(8,128)S(1)} %copy.25.gain_ref, f32[384,128]{1,0:T(8,128)S(1)} %get-tuple-element.34.cosb_ref, ...), custom_call_target="tpu_custom_call" | custom-call | flops 3600000000 | bytes 9000000 | tf_op jit(solution)/shard_map/analysis/pallas_call | solution.py:105
  15.8 1.8 copy-done.3
  17.6 1.0 copy-done.10
  18.6 11.5 %all-to-all-start = ((bf16[32,144,384]{2,1,0:T(8,128)(2,1)}), bf16[32,144,384]{2,1,0:T(8,128)(2,1)S(1)}, u32[]{:S(2)}, u32[]{:S(2)}) async-start(bf16[32,144,384]{2,1,0:T(8,128)(2,1)} %bitcast.33), calls=%async_computation | async-start | bytes 7077888 | tf_op jit(solution)/shard_map/all_to_all | solution.py:427
  30.7 20.3 %legendre_table.1.table_ref = bf16[6,392,768]{2,1,0:T(8,128)(2,1)S(1)} custom-call(f32[2,8,128]{2,1,0:T(8,128)S(1)} %broadcast_in_dim.65.orders_ref, f32[8,768]{1,0:T(8,128)S(1)} %broadcast_in_dim.66.cosine_ref, f32[8,768]{1,0:T(8,128)S(1)} %broadcast_in_dim.67.low_ref, f32[8,768]{1,0:T(8,128)S(1)} %add_multiply_fusion.start_ref), custom_call_target="tpu_custom_call" | custom-call | flops 10000000000 | bytes 4000000 | tf_op jit(solution)/shard_map/legendre_table/pallas_call | solution.py:215
  51.1 1.8 copy-done
  52.8 2.9 fusion.39
  55.7 2.2 rev.3
  58.0 55.1 %all-to-all-done = bf16[32,144,384]{2,1,0:T(8,128)(2,1)S(1)} async-done(((bf16[32,144,384]{2,1,0:T(8,128)(2,1)}), bf16[32,144,384]{2,1,0:T(8,128)(2,1)S(1)}, u32[]{:S(2)}, u32[]{:S(2)}) %all-to-all-start) | async-done | bytes 3538976 | tf_op jit(solution)/shard_map/all_to_all | solution.py:427
  113.1 2.0 copy-done.1
  115.1 3.6 forward.1
  118.7 22.0 %collective-permute-done.1 = bf16[2304,384]{1,0:T(8,128)(2,1)} collective-permute-done((bf16[2304,384]{1,0:T(8,128)(2,1)S(1)}, bf16[2304,384]{1,0:T(8,128)(2,1)}, u32[]{:S(2)}, u32[]{:S(2)}) %collective-permute-start.1) | collective-permute-done | bytes 1769504 | tf_op jit(solution)/shard_map/ppermute | solution.py:418
  140.8 4.7 %all-to-all-start.1 = ((bf16[32,72,384]{2,1,0:T(8,128)(2,1)}), bf16[32,72,384]{2,1,0:T(8,128)(2,1)S(1)}, u32[]{:S(2)}, u32[]{:S(2)}) async-start(bf16[32,72,384]{2,1,0:T(8,128)(2,1)} %bitcast.10), calls=%async_computation.1 | async-start | bytes 3538944 | tf_op jit(solution)/shard_map/all_to_all | solution.py:427
  145.5 5.3 %collective-permute-start.2 = (bf16[6,192,384]{2,1,0:T(8,128)(2,1)}, bf16[6,192,384]{2,1,0:T(8,128)(2,1)S(1)}, u32[]{:S(2)}, u32[]{:S(2)}) collective-permute-start(bf16[6,192,384]{2,1,0:T(8,128)(2,1)} %rev.3), channel_id=1, source_target_pairs={{0,31},{1,30},{2,29},{3,28},{4,27},{5,26},{6,25},{7,24},{8,23},{9,... | collective-permute-start | bytes 2654216 | tf_op jit(solution)/shard_map/ppermute | solution.py:423
  151.4 74.2 %collective-permute-done.2 = bf16[6,192,384]{2,1,0:T(8,128)(2,1)S(1)} collective-permute-done((bf16[6,192,384]{2,1,0:T(8,128)(2,1)}, bf16[6,192,384]{2,1,0:T(8,128)(2,1)S(1)}, u32[]{:S(2)}, u32[]{:S(2)}) %collective-permute-start.2) | collective-permute-done | bytes 884768 | tf_op jit(solution)/shard_map/ppermute | solution.py:423
  225.9 1.6 maximum_maximum_fusion.1.other_ref
  228.1 1.5 copy-done.4
  230.3 7.8 %mixing.1 = (bf16[32,72,384]{2,1,0:T(8,128)(2,1)S(1)}, f32[8,384]{1,0:T(8,128)S(1)}) custom-call(s32[1]{0:T(128)} %bitcast.7.rank_ref, bf16[32,72,384]{2,1,0:T(8,128)(2,1)S(1)} %all-to-all-done.1.coeffs_ref, bf16[6,384,384]{2,1,0:T(8,128)(2,1)S(1)} %maximum_maximum_fusion.own_ref, bf16[6,384,384]{2,1,0:T(8,128)(2,1)S(1)} %copy-done.4, f32[8,384]{1,0:T(8,128)S(1)} %copy-done.9), custom_call_target="tpu_custom_call" | custom-call | flops 2700000000 | bytes 7000000 | tf_op jit(solution)/shard_map/mixing/pallas_call | solution.py:307
  238.1 48.5 %all_to_all.20 = bf16[32,72,384]{2,1,0:T(8,128)(2,1)S(1)} all-to-all(bf16[32,72,384]{2,1,0:T(8,128)(2,1)S(1)} %get-tuple-element.22), channel_id=1, replica_groups=mesh['section'=8,'sp'=32] {'sp'}, dimensions={0} | all-to-all | bytes 3538944 | tf_op jit(solution)/shard_map/all_to_all | solution.py:427
  286.6 5.6 %inverse.1 = bf16[32,6,24,384]{3,2,1,0:T(8,128)(2,1)} custom-call(bf16[6,392,768]{2,1,0:T(8,128)(2,1)S(1)} %copy-done.2, bf16[2304,384]{1,0:T(8,128)(2,1)S(1)} %bitcast.32, f32[8,384]{1,0:T(8,128)S(1)} %get-tuple-element.23.diag_ref), custom_call_target="tpu_custom_call" | custom-call | flops 1400000000 | bytes 9000000 | tf_op jit(solution)/shard_map/inverse/pallas_call | solution.py:341
  292.2 4.9 %all-to-all-start.3 = ((bf16[32,144,384]{2,1,0:T(8,128)(2,1)}), bf16[32,144,384]{2,1,0:T(8,128)(2,1)S(1)}, u32[]{:S(2)}, u32[]{:S(2)}) async-start(bf16[32,144,384]{2,1,0:T(8,128)(2,1)} %bitcast.12), calls=%async_computation.3 | async-start | bytes 7077888 | tf_op jit(solution)/shard_map/all_to_all | solution.py:427
  297.2 1.7 copy.26
  299.0 1.6 collective-permute-start.7
  300.6 37.7 %collective-permute-done.5 = bf16[1,192]{1,0:T(2,128)(2,1)S(1)} collective-permute-done((bf16[1,192]{1,0:T(2,128)(2,1)S(1)}, bf16[1,192]{1,0:T(2,128)(2,1)S(1)}, u32[]{:S(2)}, u32[]{:S(2)}) %collective-permute-start.5) | collective-permute-done | bytes 416 | tf_op jit(solution)/shard_map/ppermute | solution.py:418
  339.1 1.3 collective-permute-done.7
  342.0 37.7 %all-to-all-done.3 = bf16[32,144,384]{2,1,0:T(8,128)(2,1)S(1)} async-done(((bf16[32,144,384]{2,1,0:T(8,128)(2,1)}), bf16[32,144,384]{2,1,0:T(8,128)(2,1)S(1)}, u32[]{:S(2)}, u32[]{:S(2)}) %all-to-all-start.3) | async-done | bytes 3538976 | tf_op jit(solution)/shard_map/all_to_all | solution.py:427
  379.7 0.9 copy-done.5
  380.6 0.9 copy-done.6
  381.5 1.3 copy-done.11
  382.8 17.2 %synthesis.1 = bf16[12,192,768]{2,1,0:T(8,128)(2,1)} custom-call(bf16[4608,384]{1,0:T(8,128)(2,1)S(1)} %bitcast.34, bf16[12,192,768]{2,1,0:T(8,128)(2,1)} %collective-permute-done.4.field_ref, bf16[2,384,768]{2,1,0:T(8,128)(2,1)S(1)} %copy-done.11, f32[192,1]{1,0:T(8,128)S(1)} %copy-done.6, bf16[384,192]{1,0:T(8,128)(2,1)} %bitcast.16.up_ref, ...), custom_call_target="tpu_custom_call" | custom-call | flops 8000000000 | bytes 12000000 | tf_op jit(solution)/shard_map/synthesis/pallas_call | solution.py:388
  (73 shorter events, 7.5 us)
Async XLA Ops:
  3.2 2.0 copy-start.7
  15.8 1.8 copy-start.3
  17.6 1.0 copy-start.10
  18.6 94.4 %all-to-all-start = ((bf16[32,144,384]{2,1,0:T(8,128)(2,1)}), bf16[32,144,384]{2,1,0:T(8,128)(2,1)S(1)}, u32[]{:S(2)}, u32[]{:S(2)}) async-start(bf16[32,144,384]{2,1,0:T(8,128)(2,1)} %bitcast.33), calls=%async_computation | async-start | bytes 7077888 | tf_op jit(solution)/shard_map/all_to_all | solution.py:427
  30.1 22.7 %collective-permute-start = (bf16[12,192,384]{2,1,0:T(8,128)(2,1)}, bf16[12,192,384]{2,1,0:T(8,128)(2,1)}, u32[]{:S(2)}, u32[]{:S(2)}) collective-permute-start(bf16[12,192,384]{2,1,0:T(8,128)(2,1)} %bitcast.37), channel_id=1, source_target_pairs={{0,32},{32,64},{64,96},{96,128},{128,160},{160,192},{192,224},{224... | collective-permute-start | bytes 5308424 | tf_op jit(solution)/shard_map/ppermute | solution.py:418
  51.1 1.8 copy-start
  113.0 2.0 copy-start.1
  118.7 22.1 %collective-permute-start.1 = (bf16[2304,384]{1,0:T(8,128)(2,1)S(1)}, bf16[2304,384]{1,0:T(8,128)(2,1)}, u32[]{:S(2)}, u32[]{:S(2)}) collective-permute-start(bf16[2304,384]{1,0:T(8,128)(2,1)S(1)} %get-tuple-element.19), channel_id=1, source_target_pairs={{0,32},{32,64},{64,96},{96,128},{128,160},{160,192},{192,224},{224... | collective-permute-start | bytes 5308424 | tf_op jit(solution)/shard_map/ppermute | solution.py:418
  140.8 10.0 %copy-start.12 = (bf16[6,192,384]{2,1,0:T(8,128)(2,1)S(1)}, bf16[6,192,384]{2,1,0:T(8,128)(2,1)}, u32[]{:S(2)}) copy-start(bf16[6,192,384]{2,1,0:T(8,128)(2,1)} %get-tuple-element.25) | copy-start | bytes 2654212
  140.8 87.3 %all-to-all-start.1 = ((bf16[32,72,384]{2,1,0:T(8,128)(2,1)}), bf16[32,72,384]{2,1,0:T(8,128)(2,1)S(1)}, u32[]{:S(2)}, u32[]{:S(2)}) async-start(bf16[32,72,384]{2,1,0:T(8,128)(2,1)} %bitcast.10), calls=%async_computation.1 | async-start | bytes 3538944 | tf_op jit(solution)/shard_map/all_to_all | solution.py:427
  145.5 5.5 %copy-start.13 = (bf16[6,192,384]{2,1,0:T(8,128)(2,1)S(1)}, bf16[6,192,384]{2,1,0:T(8,128)(2,1)}, u32[]{:S(2)}) copy-start(bf16[6,192,384]{2,1,0:T(8,128)(2,1)} %get-tuple-element.25) | copy-start | bytes 2654212
  145.5 80.1 %collective-permute-start.2 = (bf16[6,192,384]{2,1,0:T(8,128)(2,1)}, bf16[6,192,384]{2,1,0:T(8,128)(2,1)S(1)}, u32[]{:S(2)}, u32[]{:S(2)}) collective-permute-start(bf16[6,192,384]{2,1,0:T(8,128)(2,1)} %rev.3), channel_id=1, source_target_pairs={{0,31},{1,30},{2,29},{3,28},{4,27},{5,26},{6,25},{7,24},{8,23},{9,... | collective-permute-start | bytes 2654216 | tf_op jit(solution)/shard_map/ppermute | solution.py:423
  151.4 76.0 %collective-permute-start.3 = (f32[8,384]{1,0:T(8,128)S(1)}, f32[8,384]{1,0:T(8,128)S(1)}, u32[]{:S(2)}, u32[]{:S(2)}) collective-permute-start(f32[8,384]{1,0:T(8,128)S(1)} %get-tuple-element.21), channel_id=1, source_target_pairs={{0,32},{32,64},{64,96},{96,128},{128,160},{160,192},{192,224},{224... | collective-permute-start | bytes 36872 | tf_op jit(solution)/shard_map/ppermute | solution.py:418
  227.5 0.6 copy-start.8
  228.1 1.5 copy-start.4
  229.5 0.7 copy-start.9
  230.3 56.3 %copy-start.2 = (bf16[6,392,768]{2,1,0:T(8,128)(2,1)S(1)}, bf16[6,392,768]{2,1,0:T(8,128)(2,1)}, u32[]{:S(2)}) copy-start(bf16[6,392,768]{2,1,0:T(8,128)(2,1)} %copy-done) | copy-start | bytes 10838020
  292.2 4.9 %copy-start.15 = (bf16[1,192]{1,0:T(2,128)(2,1)S(1)}, bf16[1,192]{1,0:T(2,128)(2,1)}, u32[]{:S(2)}) copy-start(bf16[1,192]{1,0:T(2,128)(2,1)} %param.10) | copy-start | bytes 1156
  292.2 6.8 %copy-start.14 = (bf16[1,384]{1,0:T(2,128)(2,1)S(1)}, bf16[1,384]{1,0:T(2,128)(2,1)}, u32[]{:S(2)}) copy-start(bf16[1,384]{1,0:T(2,128)(2,1)} %param.12) | copy-start | bytes 2308
  292.2 87.5 %all-to-all-start.3 = ((bf16[32,144,384]{2,1,0:T(8,128)(2,1)}), bf16[32,144,384]{2,1,0:T(8,128)(2,1)S(1)}, u32[]{:S(2)}, u32[]{:S(2)}) async-start(bf16[32,144,384]{2,1,0:T(8,128)(2,1)} %bitcast.12), calls=%async_computation.3 | async-start | bytes 7077888 | tf_op jit(solution)/shard_map/all_to_all | solution.py:427
  297.1 45.0 %collective-permute-start.4 = (bf16[12,192,768]{2,1,0:T(8,128)(2,1)}, bf16[12,192,768]{2,1,0:T(8,128)(2,1)}, u32[]{:S(2)}, u32[]{:S(2)}) collective-permute-start(bf16[12,192,768]{2,1,0:T(8,128)(2,1)} %bitcast.35), channel_id=1, source_target_pairs={{0,32},{32,64},{64,96},{96,128},{128,160},{160,192},{192,224},{224... | collective-permute-start | bytes 10616840 | tf_op jit(solution)/shard_map/ppermute | solution.py:418
  297.1 41.2 %collective-permute-start.5 = (bf16[1,192]{1,0:T(2,128)(2,1)S(1)}, bf16[1,192]{1,0:T(2,128)(2,1)S(1)}, u32[]{:S(2)}, u32[]{:S(2)}) collective-permute-start(bf16[1,192]{1,0:T(2,128)(2,1)S(1)} %copy-done.15), channel_id=1, source_target_pairs={{0,32},{32,64},{64,96},{96,128},{128,160},{160,192},{192,224},{224... | collective-permute-start | bytes 1160 | tf_op jit(solution)/shard_map/ppermute | solution.py:418
  298.9 42.3 %collective-permute-start.6 = (bf16[1,192,384]{1,2,0:T(8,128)(2,1)}, bf16[1,192,384]{1,2,0:T(8,128)(2,1)}, u32[]{:S(2)}, u32[]{:S(2)}) collective-permute-start(bf16[1,192,384]{1,2,0:T(8,128)(2,1)} %copy.26), channel_id=1, source_target_pairs={{0,32},{32,64},{64,96},{96,128},{128,160},{160,192},{192,224},{224... | collective-permute-start | bytes 442376 | tf_op jit(solution)/shard_map/ppermute | solution.py:418
  299.0 41.4 %collective-permute-start.7 = (bf16[1,384]{1,0:T(2,128)(2,1)S(1)}, bf16[1,384]{1,0:T(2,128)(2,1)S(1)}, u32[]{:S(2)}, u32[]{:S(2)}) collective-permute-start(bf16[1,384]{1,0:T(2,128)(2,1)S(1)} %copy-done.14), channel_id=1, source_target_pairs={{0,32},{32,64},{64,96},{96,128},{128,160},{160,192},{192,224},{224... | collective-permute-start | bytes 2312 | tf_op jit(solution)/shard_map/ppermute | solution.py:418
  300.6 41.5 %collective-permute-start.8 = (bf16[1,192,384]{2,1,0:T(8,128)(2,1)}, bf16[1,192,384]{2,1,0:T(8,128)(2,1)}, u32[]{:S(2)}, u32[]{:S(2)}) collective-permute-start(bf16[1,192,384]{2,1,0:T(8,128)(2,1)} %param.13), channel_id=1, source_target_pairs={{0,32},{32,64},{64,96},{96,128},{128,160},{160,192},{192,224},{224... | collective-permute-start | bytes 442376 | tf_op jit(solution)/shard_map/ppermute | solution.py:418
  379.7 0.9 copy-start.5
  380.6 0.9 copy-start.6
  381.5 1.3 copy-start.11

commit v2 on v1

v2 whole, which is shorter than its diff:
```python
import functools
import math

import jax
import jax.numpy as jnp
from jax import lax
from jax.experimental import pallas as pl
from jax.experimental.pallas import tpu as pltpu
from jax.sharding import PartitionSpec as P


C = 192
HID = 384
NLAT = 384
NLON = 768
LMAX = 384
MMAX = 384
SP = 32
ROWS = NLAT // SP
PAIRS = LMAX // SP // 2
K2 = 2 * C
BLOCK_M = 2 * PAIRS * ROWS
BLOCK_L = 2 * PAIRS * PAIRS
EARLY = 2
T_ROWS = LMAX
T_PAD = T_ROWS + 8
LANES = 2 * NLAT

EPSILON = 1e-05
SCALE_LOG2 = 64.0
DOWN = 2.0**-64
LIMIT = 2.0**32

F32 = jnp.float32
BF16 = jnp.bfloat16


def pair_low(pair):
    degree = pair + pair // PAIRS * PAIRS
    return jnp.minimum(degree, LMAX - 1 - degree)


def pair_high(pair):
    degree = pair + pair // PAIRS * PAIRS
    return jnp.maximum(degree, LMAX - 1 - degree)


def params(mebibytes):
    return pltpu.CompilerParams(vmem_limit_bytes=mebibytes * 1024 * 1024)


def in_hbm(value):
    return pltpu.with_memory_space_constraint(value, pltpu.HBM)


IN_VMEM = pl.BlockSpec(memory_space=pltpu.VMEM)


def whole(shape):
    return pl.BlockSpec(shape, lambda *_: (0,) * len(shape))


def norm_rows(values, gain):
    average = jnp.mean(values, axis=0, keepdims=True)
    centred = values - average
    variance = jnp.mean(centred * centred, axis=0, keepdims=True)
    return centred * lax.rsqrt(variance + EPSILON) * gain


def remainder(values, by):
    return values - by * jnp.floor(values * (1.0 / by))


def fill_fourier_table(table_ref, scale):
    row = lax.broadcasted_iota(jnp.int32, (MMAX, 128), 0)
    pair = lax.shift_right_logical(row, 1)
    order = jnp.where(lax.bitwise_and(row, 1) == 0, pair_low(pair), pair_high(pair)).astype(F32)
    lane = lax.broadcasted_iota(jnp.int32, (MMAX, 128), 1).astype(F32)
    angle = remainder(order * lane, float(NLON)) * (2.0 * math.pi / NLON)
    factor = jnp.where(order == 0.0, 1.0, scale)
    cosine, sine = jnp.cos(angle) * factor, jnp.sin(angle) * factor
    sixth = jnp.floor(remainder(order, 6.0) + 0.5)
    half = jnp.where((sixth == 1.0) | (sixth == 5.0), 0.5, -0.5)
    turn_cos = jnp.where(sixth == 0.0, 1.0, jnp.where(sixth == 3.0, -1.0, half))
    root = math.sqrt(0.75)
    turn_sin = jnp.where((sixth == 0.0) | (sixth == 3.0), 0.0, jnp.where(sixth < 3.0, root, -root))
    for part in range(NLON // 128):
        lanes = slice(128 * part, 128 * part + 128)
        table_ref[0:MMAX, lanes] = cosine.astype(BF16)
        table_ref[MMAX : 2 * MMAX, lanes] = (-sine).astype(BF16)
        cosine, sine = cosine * turn_cos - sine * turn_sin, sine * turn_cos + cosine * turn_sin


def cycle_weights(rank):
    cycle = lax.broadcasted_iota(jnp.int32, (16, 256), 0) + rank * ROWS
    term = (lax.broadcasted_iota(jnp.int32, (16, 256), 1) + 1).astype(F32)
    turns = remainder(term * (2 * cycle + 1).astype(F32), 2.0 * NLAT)
    parts = jnp.cos(turns * (math.pi / NLAT)) / (4.0 * term * term - 1.0)
    series = jnp.sum(jnp.where(term <= NLAT // 2, parts, 0.0), axis=1, keepdims=True)
    return 2.0 / NLAT * (1.0 - 2.0 * series) * (2.0 * math.pi / NLON)


def analysis_kernel(
    rank_ref, field_ref, gain_ref, out_ref, table_ref, weight_ref, column_ref, normed_ref, acc_ref
):
    step = pl.program_id(0)

    @pl.when(step == 0)
    def _():
        for half in range(2):
            normed_ref[half, 0:64] = jnp.zeros((64, NLON), BF16)
            normed_ref[half, 256:320] = jnp.zeros((64, NLON), BF16)
        fill_fourier_table(table_ref, 1.0)
        weight_ref[...] = jnp.broadcast_to(cycle_weights(rank_ref[0]), (16, 128))
        same = lax.broadcasted_iota(jnp.int32, (C, C), 0) == lax.broadcasted_iota(jnp.int32, (C, C), 1)
        column = jnp.sum(jnp.where(same, gain_ref[...].astype(F32), 0.0), axis=1, keepdims=True)
        column_ref[...] = jnp.broadcast_to(column, (C, 128))

    @pl.when(step < ROWS // 2)
    def _():
        dims = (((1,), (1,)), ((), ()))
        gain = jnp.concatenate([column_ref[...]] * (NLON // 128), axis=1)
        for half in range(2):
            normed_ref[half, 64:256] = norm_rows(field_ref[half].astype(F32), gain).astype(BF16)
        for half in range(2):
            cycle = 2 * step + half
            weight = weight_ref[pl.ds(cycle, 1), :]
            rows = pl.ds(cycle, MMAX, stride=ROWS)
            real = lax.dot_general(
                table_ref[0:MMAX], normed_ref[half, 64:320], dims, preferred_element_type=F32
            )
            imag = lax.dot_general(
                table_ref[MMAX : 2 * MMAX], normed_ref[half, 0:256], dims, preferred_element_type=F32
            )
            acc_ref[0, rows, :] = real[:, 0:128] * weight
            acc_ref[1, rows, :] = (real[:, 128:256] + imag[:, 0:128]) * weight
            acc_ref[2, rows, :] = imag[:, 128:256] * weight

    @pl.when(step >= ROWS // 2)
    def _():
        base = (step - ROWS // 2) * (MMAX * ROWS // 6)

        @pl.loop(0, MMAX * ROWS // 6 // 128)
        def _(piece):
            into = pl.ds(pl.multiple_of(piece * 128, 128), 128)
            rows = pl.ds(pl.multiple_of(base + piece * 128, 128), 128)
            for part in range(3):
                out_ref[into, 128 * part : 128 * part + 128] = acc_ref[part, rows, :].astype(BF16)


def analysis(rank, field, gain):
    steps = ROWS // 2
    return pl.pallas_call(
        analysis_kernel,
        grid=(steps + 6,),
        in_specs=[
            pl.BlockSpec(memory_space=pltpu.SMEM),
            pl.BlockSpec((2, C, NLON), lambda j: (jnp.minimum(j, steps - 1), 0, 0)),
            whole((1, C)),
        ],
        out_specs=pl.BlockSpec((MMAX * ROWS // 6, K2), lambda j: (jnp.maximum(j - steps, 0), 0)),
        out_shape=pltpu.HBM((MMAX * ROWS, K2), BF16),
        scratch_shapes=[
            pltpu.VMEM((2 * MMAX, NLON), BF16),
            pltpu.VMEM((16, 128), F32),
            pltpu.VMEM((C, 128), F32),
            pltpu.VMEM((2, 320, NLON), BF16),
            pltpu.VMEM((3, MMAX * ROWS, 128), F32),
        ],
        compiler_params=params(28),
        cost_estimate=pl.CostEstimate(flops=3_600_000_000, bytes_accessed=9_000_000, transcendentals=0),
        name="analysis",
    )(rank, in_hbm(field), gain)


def legendre_kernel(orders_ref, cosine_ref, low_ref, start_ref, out_ref, fourier_ref, acc_ref, diag_ref):
    step = pl.program_id(0)

    @pl.when(step == 0)
    def _():
        fill_fourier_table(fourier_ref, 2.0)
        order = [orders_ref[0], orders_ref[1]]
        order_sq = [order[0] * order[0], order[1] * order[1]]
        cosine = cosine_ref[...]
        is_low = low_ref[...] > 0.5
        start = start_ref[...]
        start_level = jnp.floor(start * (1.0 / SCALE_LOG2) + 0.5)
        start_lead = jnp.exp2(start - SCALE_LOG2 * start_level)

        def spread(pair):
            return jnp.where(
                is_low,
                jnp.concatenate([pair[0]] * (LANES // 128), axis=1),
                jnp.concatenate([pair[1]] * (LANES // 128), axis=1),
            )

        order_lanes = spread(order)

        def advance(degree_index, state):
            lead, lag, level = state
            degree = degree_index.astype(F32)
            degree_sq = degree * degree
            degree_norm = jnp.maximum(4.0 * degree_sq - 1.0, 0.0)
            before_sq = (degree - 1.0) * (degree - 1.0)
            before_norm = jnp.maximum(4.0 * before_sq - 1.0, 1.0)
            leading, trailing = [], []
            for one_sq in order_sq:
                lead_coeff = jnp.sqrt(degree_norm / jnp.maximum(degree_sq - one_sq, 1.0))
                leading.append(lead_coeff)
                trailing.append(lead_coeff * jnp.sqrt(jnp.maximum(before_sq - one_sq, 0.0) / before_norm))
            following = spread(leading) * cosine * lead - spread(trailing) * lag
            first = order_lanes == degree
            lag = jnp.where(first, 0.0, lead)
            lead = jnp.where(first, start_lead, following)
            level = jnp.where(first, start_level, level)
            large = jnp.abs(lead) > LIMIT
            lead = jnp.where(large, lead * DOWN, lead)
            lag = jnp.where(large, lag * DOWN, lag)
            level = jnp.where(large, level + 1.0, level)
            value = lead * jnp.where(level > -0.5, 1.0, DOWN)
            value = value * jnp.where(level > -1.5, 1.0, jnp.where(level > -2.5, DOWN, 0.0))
            return (lead, lag, level), value, first

        def position(degree_index):
            mirrored = lax.rem(degree_index, 2 * PAIRS) >= PAIRS
            degree = jnp.where(mirrored, LMAX - 1 - degree_index, degree_index)
            pair = degree - degree // (2 * PAIRS) * PAIRS
            return pl.multiple_of(pair * 16, 16)

        def lower(degree_index, state):
            state, value, _ = advance(degree_index, state)
            rows = pl.ds(position(degree_index) + 8, 8)
            low = jnp.where(is_low, value, 0.0)
            for part in range(LANES // 128):
                acc_ref[part, rows, :] = low[:, 128 * part : 128 * part + 128]
            return state

        def upper(degree_index, state):
            state, value, first = advance(degree_index, state)
            base = position(degree_index)
            low = jnp.where(is_low, value, 0.0)
            high = jnp.where(is_low, 0.0, value)
            added = jnp.where(first, 0.0, high)
            for part in range(LANES // 128):
                lanes = slice(128 * part, 128 * part + 128)
                acc_ref[part, pl.ds(base, 8), :] = low[:, lanes]
                acc_ref[part, pl.ds(base + 8, 8), :] += added[:, lanes]
            diag_ref[...] += jnp.where(first, high, 0.0)
            return state

        diag_ref[...] = jnp.zeros_like(diag_ref)
        zero = jnp.zeros((8, LANES), F32)
        state = lax.fori_loop(0, LMAX // 2, lower, (zero, zero, zero))
        lax.fori_loop(LMAX // 2, LMAX, upper, state)

    for part in range(LANES // 128):
        rows = acc_ref[part, pl.ds(step, T_ROWS, stride=8), :]
        out_ref[0:T_ROWS, 128 * part : 128 * part + 128] = rows.astype(BF16)
    row = lax.broadcasted_iota(jnp.int32, (8, LANES), 0)
    out_ref[T_ROWS:T_PAD] = jnp.where(row == 0, diag_ref[pl.ds(step, 1), :], 0.0).astype(BF16)


def legendre_table(orders, cosine, low, start):
    return pl.pallas_call(
        legendre_kernel,
        grid=(PAIRS,),
        in_specs=[whole((2, 8, 128)), whole((8, LANES)), whole((8, LANES)), whole((8, LANES))],
        out_specs=[
            pl.BlockSpec((None, T_PAD, LANES), lambda i: (i, 0, 0)),
            whole((2 * MMAX, NLON)),
        ],
        out_shape=[pltpu.HBM((PAIRS, T_PAD, LANES), BF16), pltpu.HBM((2 * MMAX, NLON), BF16)],
        scratch_shapes=[pltpu.VMEM((LANES // 128, T_ROWS * 8, 128), F32), pltpu.VMEM((8, LANES), F32)],
        compiler_params=params(22),
        cost_estimate=pl.CostEstimate(flops=10_000_000_000, bytes_accessed=4_000_000, transcendentals=0),
        name="legendre_table",
    )(orders, cosine, low, start)


def forward_kernel(first, count, table_ref, spectral_ref, out_ref, diag_ref, acc_ref):
    step = pl.program_id(0)
    values = spectral_ref[:, first + step].reshape(LANES, K2)
    result = jnp.dot(table_ref[...], values, preferred_element_type=F32)
    for part in range(3):
        acc_ref[part, pl.ds(step, T_ROWS, stride=count), :] = result[0:T_ROWS, 128 * part : 128 * part + 128]
    row = lax.broadcasted_iota(jnp.int32, (8, K2), 0)

    @pl.when(step == 0)
    def _():
        diag_ref[...] = jnp.zeros_like(diag_ref)

    diag_ref[...] = jnp.where(row == first + step, result[T_ROWS : T_ROWS + 1], diag_ref[...])

    @pl.when(step == count - 1)
    def _():
        @pl.loop(0, T_ROWS * count // 256)
        def _(piece):
            rows = pl.ds(pl.multiple_of(piece * 256, 256), 256)
            for part in range(3):
                out_ref[rows, 128 * part : 128 * part + 128] = acc_ref[part, rows, :].astype(BF16)


def forward(table, spectral, first, count):
    return pl.pallas_call(
        functools.partial(forward_kernel, first, count),
        grid=(count,),
        in_specs=[pl.BlockSpec((None, T_PAD, LANES), lambda i: (first + i, 0, 0)), IN_VMEM],
        out_specs=[whole((T_ROWS * count, K2)), whole((8, K2))],
        out_shape=[pltpu.HBM((T_ROWS * count, K2), BF16), jax.ShapeDtypeStruct((8, K2), F32)],
        scratch_shapes=[pltpu.VMEM((3, T_ROWS * count, 128), F32)],
        compiler_params=params(14),
        cost_estimate=pl.CostEstimate(
            flops=230_000_000 * count, bytes_accessed=1_500_000 * count, transcendentals=0
        ),
        name="forward",
    )(in_hbm(table), spectral)


def mixing_choice(rank, first, count):
    block = 4 * count
    step = jnp.arange(PAIRS // 2, dtype=jnp.int32)[:, None]
    index = jnp.arange(SP * block, dtype=jnp.int32)[None, :]
    within = index % block
    local = within // (2 * count)
    second = within // count % 2
    order = pair_low(index // block * PAIRS + first + within % count)
    low_degree = pair_low(rank * PAIRS + 2 * step + local)
    uses_low = jnp.logical_and(second == 1, order <= low_degree)
    uses_own = uses_low == (rank < SP // 2)
    choice = (2 * local + uses_own.astype(jnp.int32)).astype(F32)
    return jnp.broadcast_to(choice[:, :, None], (PAIRS // 2, SP * block, 128))


def mixing_kernel(count, rank_ref, coeffs_ref, choice_ref, own_ref, other_ref, diag_ref, *refs):
    out_ref, diag_out_ref = refs[-2:]
    step = pl.program_id(0)
    block = 4 * count
    values = coeffs_ref[:, pl.ds(pl.multiple_of(block * step, 8), block), :].reshape(SP * block, K2)
    choice = jnp.concatenate([choice_ref[...]] * (K2 // 128), axis=1)
    result = []
    for pair in range(2):
        own = jnp.dot(values, own_ref[2 * step + pair], preferred_element_type=F32)
        other = jnp.dot(values, other_ref[PAIRS - 1 - 2 * step - pair], preferred_element_type=F32)
        result.append(jnp.where(choice == 2.0 * pair, other, own))
    mixed = jnp.where(choice < 1.5, result[0], result[1]).astype(BF16)
    out_ref[...] = mixed.reshape(SP, block, K2)

    if len(refs) == 2:
        own_is_low = rank_ref[0] < SP // 2

        @pl.when(step == 0)
        def _():
            diag_out_ref[...] = jnp.zeros_like(diag_out_ref)

        diag = diag_ref[...].astype(BF16)
        row = lax.broadcasted_iota(jnp.int32, (8, K2), 0)
        for pair in range(2):
            own = jnp.dot(diag, own_ref[2 * step + pair], preferred_element_type=F32)
            other = jnp.dot(diag, other_ref[PAIRS - 1 - 2 * step - pair], preferred_element_type=F32)
            chosen = jnp.where(own_is_low, other, own)
            diag_out_ref[...] = jnp.where(row == 2 * step + pair, chosen, diag_out_ref[...])
    else:
        diag_out_ref[...] = diag_ref[...]


def mixing(rank, coeffs, choice, own, other, diag, count, offset, filled=None):
    block = 4 * count
    extra = [] if filled is None else [filled]
    return pl.pallas_call(
        functools.partial(mixing_kernel, count),
        grid=(PAIRS // 2,),
        in_specs=[
            pl.BlockSpec(memory_space=pltpu.SMEM),
            IN_VMEM,
            pl.BlockSpec((None, SP * block, 128), lambda g: (g, 0, 0)),
            IN_VMEM,
            IN_VMEM,
            whole((8, K2)),
        ]
        + [pl.BlockSpec(memory_space=pl.ANY) for _ in extra],
        out_specs=[pl.BlockSpec((SP, block, K2), lambda g: (0, offset // block + g, 0)), whole((8, K2))],
        out_shape=[pltpu.HBM((SP, BLOCK_L, K2), BF16), jax.ShapeDtypeStruct((8, K2), F32)],
        input_output_aliases={6: 0} if extra else {},
        compiler_params=params(14),
        cost_estimate=pl.CostEstimate(
            flops=450_000_000 * count, bytes_accessed=1_200_000 * count, transcendentals=0
        ),
        name="mixing",
    )(rank, coeffs, in_hbm(choice), own, other, diag, *extra)


def inverse_kernel(table_ref, mixed_ref, diag_ref, out_ref, early_ref, late_ref, values_ref):
    step = pl.program_id(0)
    split = BLOCK_L // PAIRS * (PAIRS - EARLY)
    rest = BLOCK_L - split

    @pl.when(step == 0)
    def _():
        @pl.loop(0, SP)
        def _(owner):
            early = pl.ds(pl.multiple_of(owner * split, 8), split)
            late = pl.ds(pl.multiple_of(owner * rest, 8), rest)
            for part in range(3):
                lanes = slice(128 * part, 128 * part + 128)
                early_ref[part, early, :] = mixed_ref[owner, 0:split, lanes].astype(F32)
                late_ref[part, late, :] = mixed_ref[owner, split:BLOCK_L, lanes].astype(F32)

    @pl.when(step < EARLY)
    def _():
        rows = pl.ds(step, T_ROWS, stride=EARLY)
        for part in range(3):
            values_ref[:, 128 * part : 128 * part + 128] = late_ref[part, rows, :].astype(BF16)

    @pl.when(step >= EARLY)
    def _():
        rows = pl.ds(step - EARLY, T_ROWS, stride=PAIRS - EARLY)
        for part in range(3):
            values_ref[:, 128 * part : 128 * part + 128] = early_ref[part, rows, :].astype(BF16)

    row = lax.broadcasted_iota(jnp.int32, (8, K2), 0)
    diag = jnp.where(row == 0, diag_ref[pl.ds(step, 1), :], 0.0).astype(BF16)
    dims = (((0,), (0,)), ((), ()))
    result = lax.dot_general(table_ref[step, 0:T_ROWS], values_ref[...], dims, preferred_element_type=F32)
    result += lax.dot_general(table_ref[step, T_ROWS:T_PAD], diag, dims, preferred_element_type=F32)
    out_ref[...] = result.astype(BF16).reshape(SP, 2 * ROWS, K2)


def inverse(table, mixed, diag):
    return pl.pallas_call(
        inverse_kernel,
        grid=(PAIRS,),
        in_specs=[IN_VMEM, IN_VMEM, whole((8, K2))],
        out_specs=pl.BlockSpec((SP, None, 2 * ROWS, K2), lambda i: (0, i, 0, 0)),
        out_shape=pltpu.HBM((SP, PAIRS, 2 * ROWS, K2), BF16),
        scratch_shapes=[
            pltpu.VMEM((3, T_ROWS * (PAIRS - EARLY), 128), F32),
            pltpu.VMEM((3, T_ROWS * EARLY, 128), F32),
            pltpu.VMEM((T_ROWS, K2), BF16),
        ],
        compiler_params=params(16),
        cost_estimate=pl.CostEstimate(flops=1_400_000_000, bytes_accessed=9_000_000, transcendentals=0),
        name="inverse",
    )(table, mixed, diag)


def synthesis_kernel(
    grid_ref, field_ref, table_ref, gain_ref, up_ref, bias_ref, down_ref, out_ref, acc_ref
):
    step = pl.program_id(0)

    @pl.when(step == 0)
    def _():
        @pl.loop(0, MMAX * ROWS // 256)
        def _(piece):
            rows = pl.ds(pl.multiple_of(piece * 256, 256), 256)
            for part in range(3):
                acc_ref[part, rows, :] = grid_ref[rows, 128 * part : 128 * part + 128].astype(F32)

    residuals = []
    for half in range(2):
        rows = pl.ds(2 * step + half, MMAX, stride=ROWS)
        values = jnp.concatenate([acc_ref[part, rows, :] for part in range(3)], axis=1)
        turned = values.T.astype(BF16)
        residual = field_ref[half].astype(F32)
        residual += jnp.dot(turned[0:C], table_ref[0:MMAX], preferred_element_type=F32)
        residual += jnp.dot(turned[C:K2], table_ref[MMAX : 2 * MMAX], preferred_element_type=F32)
        residuals.append(residual)
    for half in range(2):
        hidden_in = norm_rows(residuals[half], gain_ref[...]).astype(BF16)
        hidden = jnp.dot(up_ref[...], hidden_in, preferred_element_type=F32) + bias_ref[...]
        hidden = hidden * (1.0 + lax.erf(hidden * math.sqrt(0.5))) * 0.5
        branch = jnp.dot(down_ref[...], hidden.astype(BF16), preferred_element_type=F32)
        out_ref[half] = (residuals[half] + branch).astype(BF16)


def synthesis(on_grid, field, table, gain, up, bias, down):
    cycle = pl.BlockSpec((2, C, NLON), lambda j: (j, 0, 0))
    return pl.pallas_call(
        synthesis_kernel,
        grid=(ROWS // 2,),
        in_specs=[
            IN_VMEM,
            cycle,
            whole((2 * MMAX, NLON)),
            whole((C, 1)),
            whole((HID, C)),
            whole((HID, 1)),
            whole((C, HID)),
        ],
        out_specs=cycle,
        out_shape=jax.ShapeDtypeStruct((ROWS, C, NLON), BF16),
        scratch_shapes=[pltpu.VMEM((3, MMAX * ROWS, 128), F32)],
        compiler_params=params(32),
        cost_estimate=pl.CostEstimate(flops=8_000_000_000, bytes_accessed=12_000_000, transcendentals=0),
        name="synthesis",
    )(on_grid, in_hbm(field), in_hbm(table), in_hbm(gain), in_hbm(up), in_hbm(bias), in_hbm(down))


def mixing_matrix(weight):
    real_weight = weight[:, :, :C]
    imag_weight = weight[:, :, C:]
    bottom_half = jnp.concatenate([-imag_weight, real_weight], axis=2)
    return jnp.concatenate([weight, bottom_half], axis=1)


def to_next(value):
    count = lax.axis_size("section")
    return lax.ppermute(value, "section", [(i, (i + 1) % count) for i in range(count)])


def to_mirrored(value):
    count = lax.axis_size("sp")
    return lax.ppermute(value, "sp", [(d, count - 1 - d) for d in range(count)])


def to_next_mirrored(value):
    sections, count = lax.axis_size("section"), lax.axis_size("sp")
    pairs = [
        (s * count + d, (s + 1) % sections * count + count - 1 - d)
        for s in range(sections)
        for d in range(count)
    ]
    return lax.ppermute(value, ("section", "sp"), pairs)


def exchange(value):
    return lax.all_to_all(value, "sp", split_axis=0, concat_axis=0)


def legendre_inputs(rank):
    pair = rank * PAIRS + jnp.minimum(jnp.arange(8, dtype=jnp.int32), PAIRS - 1)
    orders = jnp.stack([pair_low(pair), pair_high(pair)]).astype(F32)
    lane = jnp.arange(LANES, dtype=jnp.int32)
    low = (lane // ROWS) % 2 == 0
    cycle = lane // (2 * ROWS) * ROWS + lane % ROWS
    colatitude = math.pi * (cycle.astype(F32) + 0.5) / NLAT
    steps_all = jnp.arange(1, LMAX + 1, dtype=F32)
    factors = jnp.log((2.0 * steps_all - 1.0) / (2.0 * steps_all))
    below = (steps_all <= orders[:, :, None]).astype(F32)
    partial_log = jnp.sum(below * factors, axis=2)
    start = 0.5 * jnp.log((2.0 * orders + 1.0) / (4.0 * math.pi)) + 0.5 * partial_log
    order_lanes = jnp.where(low, orders[0][:, None], orders[1][:, None])
    start = jnp.where(low, start[0][:, None], start[1][:, None])
    start = (start + order_lanes * jnp.log(jnp.sin(colatitude))) * (1.0 / math.log(2.0))
    return (
        jnp.broadcast_to(orders[:, :, None], (2, 8, 128)),
        jnp.broadcast_to(jnp.cos(colatitude), (8, LANES)),
        jnp.broadcast_to(low.astype(F32), (8, LANES)),
        start,
    )


def block(field_in, spectral_gain, spectral_weight, mixer_gain, up_weight, up_bias, down_weight):
    field = field_in[0]
    rank = lax.axis_index("sp")
    weight = spectral_weight[0]
    early_weight = to_next_mirrored(weight[PAIRS : PAIRS + 3])
    spectral = analysis(rank.reshape(1), field, spectral_gain)
    rank_after, weight, _ = lax.optimization_barrier((rank, weight, spectral))
    by_order = exchange(spectral.reshape(SP, BLOCK_M, K2))
    own_weight = to_next(weight[:PAIRS])
    late_weight = to_next(weight[PAIRS + 3 :])
    legendre, table = legendre_table(*legendre_inputs(rank_after))
    first_choice = mixing_choice(rank_after, EARLY, PAIRS - EARLY)
    second_choice = mixing_choice(rank_after, 0, EARLY)

    by_order, first_choice, second_choice = lax.optimization_barrier(
        (by_order, first_choice, second_choice)
    )
    by_order = by_order.reshape(SP, PAIRS, 2 * ROWS, K2)
    first, first_diag = forward(legendre, by_order, EARLY, PAIRS - EARLY)
    first = exchange(first.reshape(SP, -1, K2))
    second, second_diag = forward(legendre, by_order, 0, EARLY)
    second, late_weight = lax.optimization_barrier((second, late_weight))
    late_weight = to_mirrored(late_weight)
    second = to_next(second)
    first = to_next(first)
    diag = to_next(first_diag + second_diag)
    second = exchange(second.reshape(SP, -1, K2))
    other_weight = jnp.concatenate([early_weight, late_weight], axis=0)
    own_matrix, other_matrix = mixing_matrix(own_weight), mixing_matrix(other_weight)
    late = PAIRS - EARLY
    mixed, diag = mixing(
        rank.reshape(1), first, first_choice, own_matrix, other_matrix, diag, late, 0
    )
    mixed, diag = mixing(
        rank.reshape(1), second, second_choice, own_matrix, other_matrix, diag,
        EARLY, BLOCK_L // PAIRS * late, mixed
    )
    back = exchange(mixed)
    grid_part = inverse(legendre, back, diag)
    on_grid = exchange(grid_part.reshape(SP, BLOCK_M, K2))
    next_field = to_next(field)
    gain_next, bias_next = to_next(mixer_gain), to_next(up_bias)
    up_next, down_next = to_next(up_weight), to_next(down_weight)
    result = synthesis(
        on_grid.reshape(MMAX * ROWS, K2),
        next_field,
        table,
        gain_next.reshape(C, 1).astype(F32),
        up_next[0].T,
        bias_next.reshape(HID, 1).astype(F32),
        down_next[0],
    )
    return result[None]


def solution(mesh):
    in_specs = (
        P("section", "sp", None, None),
        P("section", None),
        P("section", "sp", None, None),
        P("section", None),
        P("section", None, None),
        P("section", None),
        P("section", None, None),
    )
    out_specs = P("section", "sp", None, None)
    return jax.shard_map(block, mesh=mesh, in_specs=in_specs, out_specs=out_specs, check_vma=False)
```

time: 401 us -> 366 us (0.913)
  waiting for transfers between devices: 229 us -> 172 us
  starting transfers between devices: 28.2 us -> 48.2 us
  local copies, waits for them, and re-layouts: 23.5 us -> 13.7 us
  Pallas kernels: 65.1 us -> 73.8 us
    ppermute x1, waiting for transfers between devices: 74.2 us -> 0.41 us  [to_mirrored(): return lax.ppermute(value, 'sp', [(d, count - 1 - d) for d in range(count)])]
    all_to_all x3 -> x4, waiting for transfers between devices: 92.8 us -> 116 us  [exchange(): return lax.all_to_all(value, 'sp', split_axis=0, concat_axis=0)]
    ppermute x8 -> x10, waiting for transfers between devices: 61.9 us -> 40.3 us  [to_next(): lax.ppermute(value, 'section', [(i, (i + 1) % count) for i in range(count)])]
    all_to_all x3 -> x4, starting transfers between devices: 21.1 us -> 37.2 us  [exchange(): return lax.all_to_all(value, 'sp', split_axis=0, concat_axis=0)]
    ppermute x0 -> x1, waiting for transfers between devices: none -> 15.5 us  [to_next_mirrored(): return lax.ppermute(value, ('section', 'sp'), pairs)]
    unnamed x33 -> x18, local copies, waits for them, and re-layouts: 16.2 us -> 4.52 us
    ppermute x0 -> x1, starting transfers between devices: none -> 5.33 us  [to_next_mirrored(): return lax.ppermute(value, ('section', 'sp'), pairs)]
    pallas_call x5 -> x7, Pallas kernels: 44.8 us -> 50 us  [the longest x1 13.7 us: synthesis(): pl.pallas_call(synthesis_kernel, grid=(ROWS // 2,), in_specs=[IN_VMEM, cy...]
  transfers between devices with their start and end apart: 12 -> 16, of which waited for: 7 -> 10; matrix products, arithmetic and copies ran while one was open for 3% -> 4% of each run, Pallas kernels for 5% -> 9%
where the time goes in v2:
time: 366 us; the launch traced here: 364 us
  waiting for transfers between devices  172 us (47%)
  Pallas kernels  73.8 us (20%)
  blocking collectives  50.3 us (14%)
  starting transfers between devices  48.2 us (13%)
  local copies, waits for them, and re-layouts  13.7 us (4%)
  other arithmetic  5.56 us (2%)
    all_to_all x4, waiting for transfers between devices, exchange(): return lax.all_to_all(value, 'sp', split_axis=0, concat_axis=0)  116 us
    all_to_all x1, blocking collectives, exchange(): return lax.all_to_all(value, 'sp', split_axis=0, concat_axis=0)  50.3 us
    ppermute x10, waiting for transfers between devices, to_next(): lax.ppermute(value, 'section', [(i, (i + 1) % count) for i in range(count)])  40.3 us
    all_to_all x4, starting transfers between devices, exchange(): return lax.all_to_all(value, 'sp', split_axis=0, concat_axis=0)  37.2 us
    pallas_call x1, Pallas kernels, legendre_table(): pl.pallas_call(legendre_kernel, grid=(PAIRS,), in_specs=[whole((2, 8, 128...  23.9 us
    ppermute x1, waiting for transfers between devices, to_next_mirrored(): return lax.ppermute(value, ('section', 'sp'), pairs)  15.5 us
    pallas_call x1, Pallas kernels, synthesis(): pl.pallas_call(synthesis_kernel, grid=(ROWS // 2,), in_specs=[IN_VMEM, cy...  13.7 us
    pallas_call x1, Pallas kernels, analysis(): pl.pallas_call(analysis_kernel, grid=(steps + 6,), in_specs=[pl.BlockSpec...  11.7 us
  transfers between devices with their start and end apart: 16, of which 10 were waited for; matrix products, arithmetic and copies ran while one was open for 4% of the time, Pallas kernels for 9%

profile of v2, /device:TPU:4, one launch (start us, length us, event | category | flops | bytes accessed | tf_op | source)
XLA Modules:
  0.0 363.8 jit_solution(12167120228040577265)
XLA Ops:
  0.7 11.7 %analysis.1 = bf16[4608,384]{1,0:T(8,128)(2,1)} custom-call(s32[1]{0:T(128)} %bitcast.1.rank_ref, bf16[12,192,768]{2,1,0:T(8,128)(2,1)} %bitcast.38, bf16[1,192]{1,0:T(2,128)(2,1)S(1)} %copy-done.3), custom_call_target="tpu_custom_call" | custom-call | flops 3600000000 | bytes 9000000 | tf_op jit(solution)/shard_map/analysis/pallas_call | solution.py:153
  12.4 11.5 %all-to-all-start = ((bf16[32,144,384]{2,1,0:T(8,128)(2,1)}), bf16[32,144,384]{2,1,0:T(8,128)(2,1)S(1)}, u32[]{:S(2)}, u32[]{:S(2)}) async-start(bf16[32,144,384]{2,1,0:T(8,128)(2,1)} %bitcast.34), calls=%async_computation | async-start | bytes 7077888 | tf_op jit(solution)/shard_map/all_to_all | solution.py:527
  24.8 23.9 %legendre_table.1 = (bf16[6,392,768]{2,1,0:T(8,128)(2,1)}, bf16[768,768]{1,0:T(8,128)(2,1)}) custom-call(f32[2,8,128]{2,1,0:T(8,128)S(1)} %broadcast_in_dim.76.orders_ref, f32[8,768]{1,0:T(8,128)S(1)} %broadcast_in_dim.77.cosine_ref, f32[8,768]{1,0:T(8,128)S(1)} %broadcast_in_dim.78.low_ref, f32[8,768]{1,0:T(8,128)S(1)} %add_multiply_fusion.start_ref), custom_call_target="tpu_custom_call" | custom-call | flops 10000000000 | bytes 4000000 | tf_op jit(solution)/shard_map/legendre_table/pallas_call | solution.py:264
  48.7 58.2 %all-to-all-done = bf16[32,144,384]{2,1,0:T(8,128)(2,1)S(1)} async-done(((bf16[32,144,384]{2,1,0:T(8,128)(2,1)}), bf16[32,144,384]{2,1,0:T(8,128)(2,1)S(1)}, u32[]{:S(2)}, u32[]{:S(2)}) %all-to-all-start) | async-done | bytes 3538976 | tf_op jit(solution)/shard_map/all_to_all | solution.py:527
  106.9 1.1 broadcast_in_dim.88.choice_ref
  108.9 4.9 %forward.3 = (bf16[1536,384]{1,0:T(8,128)(2,1)}, f32[8,384]{1,0:T(8,128)S(1)}) custom-call(bf16[6,392,768]{2,1,0:T(8,128)(2,1)} %get-tuple-element.23.table_ref, bf16[32,6,24,384]{3,2,1,0:T(8,128)(2,1)S(1)} %bitcast.30), custom_call_target="tpu_custom_call" | custom-call | flops 920000000 | bytes 6000000 | tf_op jit(solution)/shard_map/forward/pallas_call | solution.py:304
  113.8 4.7 %all-to-all-start.2 = ((bf16[32,48,384]{2,1,0:T(8,128)(2,1)}), bf16[32,48,384]{2,1,0:T(8,128)(2,1)}, u32[]{:S(2)}, u32[]{:S(2)}) async-start(bf16[32,48,384]{2,1,0:T(8,128)(2,1)} %bitcast.37), calls=%async_computation.2 | async-start | bytes 2359296 | tf_op jit(solution)/shard_map/all_to_all | solution.py:527
  118.5 1.1 slice.40
  119.6 2.2 slice.41
  121.8 1.3 collective-permute-start.2
  123.1 3.0 forward.2
  129.1 5.3 %collective-permute-start.3 = (bf16[3,192,384]{2,1,0:T(8,128)(2,1)S(1)}, bf16[3,192,384]{2,1,0:T(8,128)(2,1)S(1)}, u32[]{:S(2)}, u32[]{:S(2)}) collective-permute-start(bf16[3,192,384]{2,1,0:T(8,128)(2,1)S(1)} %slice_bitcast_fusion), channel_id=1, source_target_pairs={{0,63},{1,62},{2,61},{3,60},{4,59},{5,58},{6,57},{7,56},{8,55},{9,... | collective-permute-start | bytes 1327112 | tf_op jit(solution)/shard_map/ppermute | solution.py:523
  134.4 15.4 %all-to-all-done.2 = bf16[32,48,384]{2,1,0:T(8,128)(2,1)} async-done(((bf16[32,48,384]{2,1,0:T(8,128)(2,1)}), bf16[32,48,384]{2,1,0:T(8,128)(2,1)}, u32[]{:S(2)}, u32[]{:S(2)}) %all-to-all-start.2) | async-done | bytes 1179680 | tf_op jit(solution)/shard_map/all_to_all | solution.py:527
  149.9 1.5 collective-permute-start.4
  151.4 15.5 %collective-permute-done.3 = bf16[3,192,384]{2,1,0:T(8,128)(2,1)S(1)} collective-permute-done((bf16[3,192,384]{2,1,0:T(8,128)(2,1)S(1)}, bf16[3,192,384]{2,1,0:T(8,128)(2,1)S(1)}, u32[]{:S(2)}, u32[]{:S(2)}) %collective-permute-start.3) | collective-permute-done | bytes 442400 | tf_op jit(solution)/shard_map/ppermute | solution.py:523
  167.0 15.6 %all-to-all-start.1 = ((bf16[32,24,384]{2,1,0:T(8,128)(2,1)}), bf16[32,24,384]{2,1,0:T(8,128)(2,1)}, u32[]{:S(2)}, u32[]{:S(2)}) async-start(bf16[32,24,384]{2,1,0:T(8,128)(2,1)} %bitcast.9), calls=%async_computation.1 | async-start | bytes 1179648 | tf_op jit(solution)/shard_map/all_to_all | solution.py:527
  182.6 1.5 slice_negate_fusion.1
  184.0 1.6 maximum_maximum_fusion.own_ref
  187.0 1.1 constant_dynamic-update-slice_fusion
  189.0 1.6 maximum_maximum_fusion.1.other_ref
  190.6 6.5 %mixing.2 = (bf16[32,72,384]{2,1,0:T(8,128)(2,1)}, f32[8,384]{1,0:T(8,128)S(1)}) custom-call(s32[1]{0:T(128)} %bitcast.1.rank_ref, bf16[32,48,384]{2,1,0:T(8,128)(2,1)} %collective-permute-done.5.coeffs_ref, f32[3,512,128]{2,1,0:T(8,128)} %broadcast_in_dim.88.choice_ref, bf16[6,384,384]{2,1,0:T(8,128)(2,1)S(1)} %maximum_maximum_fusion.own_ref, ...), custom_call_target="tpu_custom_call" | custom-call | flops 1800000000 | bytes 4800000 | tf_op jit(solution)/shard_map/mixing/pallas_call | solution.py:369
  197.0 4.4 %all-to-all-done.1.coeffs_ref = bf16[32,24,384]{2,1,0:T(8,128)(2,1)} async-done(((bf16[32,24,384]{2,1,0:T(8,128)(2,1)}), bf16[32,24,384]{2,1,0:T(8,128)(2,1)}, u32[]{:S(2)}, u32[]{:S(2)}) %all-to-all-start.1) | async-done | bytes 589856 | tf_op jit(solution)/shard_map/all_to_all | solution.py:527
  201.5 4.2 %mixing.3 = (bf16[32,72,384]{2,1,0:T(8,128)(2,1)}, f32[8,384]{1,0:T(8,128)S(1)}) custom-call(s32[1]{0:T(128)} %bitcast.1.rank_ref, bf16[32,24,384]{2,1,0:T(8,128)(2,1)} %all-to-all-done.1.coeffs_ref, f32[3,256,128]{2,1,0:T(8,128)} %broadcast_in_dim.89.choice_ref, ...), custom_call_target="tpu_custom_call", output_to_operand_aliasing={{0}: (6, {})} | custom-call | flops 900000000 | bytes 2400000 | tf_op jit(solution)/shard_map/mixing/pallas_call | solution.py:369
  205.7 50.3 %all_to_all.25.mixed_ref = bf16[32,72,384]{2,1,0:T(8,128)(2,1)S(1)} all-to-all(bf16[32,72,384]{2,1,0:T(8,128)(2,1)} %get-tuple-element.36), channel_id=1, replica_groups=mesh['section'=8,'sp'=32] {'sp'}, dimensions={0} | all-to-all | bytes 3538944 | tf_op jit(solution)/shard_map/all_to_all | solution.py:527
  256.0 6.0 %inverse.1 = bf16[32,6,24,384]{3,2,1,0:T(8,128)(2,1)} custom-call(bf16[6,392,768]{2,1,0:T(8,128)(2,1)S(1)} %copy-done, bf16[32,72,384]{2,1,0:T(8,128)(2,1)S(1)} %all_to_all.25.mixed_ref, f32[8,384]{1,0:T(8,128)S(1)} %get-tuple-element.37.diag_ref), custom_call_target="tpu_custom_call" | custom-call | flops 1400000000 | bytes 9000000 | tf_op jit(solution)/shard_map/inverse/pallas_call | solution.py:429
  262.0 5.4 %all-to-all-start.4 = ((bf16[32,144,384]{2,1,0:T(8,128)(2,1)}), bf16[32,144,384]{2,1,0:T(8,128)(2,1)S(1)}, u32[]{:S(2)}, u32[]{:S(2)}) async-start(bf16[32,144,384]{2,1,0:T(8,128)(2,1)} %bitcast.33), calls=%async_computation.4 | async-start | bytes 7077888 | tf_op jit(solution)/shard_map/all_to_all | solution.py:527
  267.5 1.9 collective-permute-start.8
  269.4 1.7 copy.13
  271.2 37.5 %collective-permute-done.8 = bf16[1,192]{1,0:T(2,128)(2,1)S(1)} collective-permute-done((bf16[1,192]{1,0:T(2,128)(2,1)S(1)}, bf16[1,192]{1,0:T(2,128)(2,1)S(1)}, u32[]{:S(2)}, u32[]{:S(2)}) %collective-permute-start.8) | collective-permute-done | bytes 416 | tf_op jit(solution)/shard_map/ppermute | solution.py:508
  309.5 1.3 collective-permute-done.10
  312.4 37.7 %all-to-all-done.4 = bf16[32,144,384]{2,1,0:T(8,128)(2,1)S(1)} async-done(((bf16[32,144,384]{2,1,0:T(8,128)(2,1)}), bf16[32,144,384]{2,1,0:T(8,128)(2,1)S(1)}, u32[]{:S(2)}, u32[]{:S(2)}) %all-to-all-start.4) | async-done | bytes 3538976 | tf_op jit(solution)/shard_map/all_to_all | solution.py:527
  350.1 13.7 %synthesis.1 = bf16[12,192,768]{2,1,0:T(8,128)(2,1)} custom-call(bf16[4608,384]{1,0:T(8,128)(2,1)S(1)} %bitcast.32, bf16[12,192,768]{2,1,0:T(8,128)(2,1)} %collective-permute-done.7.field_ref, bf16[768,768]{1,0:T(8,128)(2,1)} %get-tuple-element.38.table_ref, f32[192,1]{1,0:T(8,128)} %copy.14.gain_ref, bf16[384,192]{1,0:T(8,128)(2,1)} %bitcast.16.up_ref, ...), custom_call_target="tpu_custom_call" | custom-call | flops 8000000000 | bytes 12000000 | tf_op jit(solution)/shard_map/synthesis/pallas_call | solution.py:478
  (66 shorter events, 10.3 us)
Async XLA Ops:
  0.0 0.7 copy-start.3
  12.4 94.4 %all-to-all-start = ((bf16[32,144,384]{2,1,0:T(8,128)(2,1)}), bf16[32,144,384]{2,1,0:T(8,128)(2,1)S(1)}, u32[]{:S(2)}, u32[]{:S(2)}) async-start(bf16[32,144,384]{2,1,0:T(8,128)(2,1)} %bitcast.34), calls=%async_computation | async-start | bytes 7077888 | tf_op jit(solution)/shard_map/all_to_all | solution.py:527
  113.8 36.1 %all-to-all-start.2 = ((bf16[32,48,384]{2,1,0:T(8,128)(2,1)}), bf16[32,48,384]{2,1,0:T(8,128)(2,1)}, u32[]{:S(2)}, u32[]{:S(2)}) async-start(bf16[32,48,384]{2,1,0:T(8,128)(2,1)} %bitcast.37), calls=%async_computation.2 | async-start | bytes 2359296 | tf_op jit(solution)/shard_map/all_to_all | solution.py:527
  119.5 7.7 %collective-permute-start = (bf16[3,192,384]{2,1,0:T(8,128)(2,1)S(1)}, bf16[3,192,384]{2,1,0:T(8,128)(2,1)S(1)}, u32[]{:S(2)}, u32[]{:S(2)}) collective-permute-start(bf16[3,192,384]{2,1,0:T(8,128)(2,1)S(1)} %slice.40), channel_id=1, source_target_pairs={{0,32},{32,64},{64,96},{96,128},{128,160},{160,192},{192,224},{224... | collective-permute-start | bytes 1327112 | tf_op jit(solution)/shard_map/ppermute | solution.py:508
  121.8 60.7 %collective-permute-start.2 = (bf16[6,192,384]{2,1,0:T(8,128)(2,1)}, bf16[6,192,384]{2,1,0:T(8,128)(2,1)}, u32[]{:S(2)}, u32[]{:S(2)}) collective-permute-start(bf16[6,192,384]{2,1,0:T(8,128)(2,1)} %slice.41), channel_id=1, source_target_pairs={{0,32},{32,64},{64,96},{96,128},{128,160},{160,192},{192,224},{224... | collective-permute-start | bytes 2654216 | tf_op jit(solution)/shard_map/ppermute | solution.py:508
  126.0 0.6 copy-start.1
  127.3 0.8 copy-start.5
  127.3 39.7 %collective-permute-start.1 = (bf16[768,384]{1,0:T(8,128)(2,1)}, bf16[768,384]{1,0:T(8,128)(2,1)}, u32[]{:S(2)}, u32[]{:S(2)}) collective-permute-start(bf16[768,384]{1,0:T(8,128)(2,1)} %get-tuple-element.27), channel_id=1, source_target_pairs={{0,32},{32,64},{64,96},{96,128},{128,160},{160,192},{192,224},{224... | collective-permute-start | bytes 1769480 | tf_op jit(solution)/shard_map/ppermute | solution.py:508
  129.1 37.8 %collective-permute-start.3 = (bf16[3,192,384]{2,1,0:T(8,128)(2,1)S(1)}, bf16[3,192,384]{2,1,0:T(8,128)(2,1)S(1)}, u32[]{:S(2)}, u32[]{:S(2)}) collective-permute-start(bf16[3,192,384]{2,1,0:T(8,128)(2,1)S(1)} %slice_bitcast_fusion), channel_id=1, source_target_pairs={{0,63},{1,62},{2,61},{3,60},{4,59},{5,58},{6,57},{7,56},{8,55},{9,... | collective-permute-start | bytes 1327112 | tf_op jit(solution)/shard_map/ppermute | solution.py:523
  149.9 40.7 %collective-permute-start.5 = (bf16[32,48,384]{2,1,0:T(8,128)(2,1)}, bf16[32,48,384]{2,1,0:T(8,128)(2,1)}, u32[]{:S(2)}, u32[]{:S(2)}) collective-permute-start(bf16[32,48,384]{2,1,0:T(8,128)(2,1)} %all-to-all-done.2), channel_id=1, source_target_pairs={{0,32},{32,64},{64,96},{96,128},{128,160},{160,192},{192,224},{224... | collective-permute-start | bytes 3538952 | tf_op jit(solution)/shard_map/ppermute | solution.py:508
  149.9 37.1 %collective-permute-start.4 = (bf16[3,192,384]{2,1,0:T(8,128)(2,1)}, bf16[3,192,384]{2,1,0:T(8,128)(2,1)}, u32[]{:S(2)}, u32[]{:S(2)}) collective-permute-start(bf16[3,192,384]{2,1,0:T(8,128)(2,1)} %copy-done.5), channel_id=1, source_target_pairs={{0,31},{1,30},{2,29},{3,28},{4,27},{5,26},{6,25},{7,24},{8,23},{9,... | collective-permute-start | bytes 1327112 | tf_op jit(solution)/shard_map/ppermute | solution.py:513
  167.0 34.5 %all-to-all-start.1 = ((bf16[32,24,384]{2,1,0:T(8,128)(2,1)}), bf16[32,24,384]{2,1,0:T(8,128)(2,1)}, u32[]{:S(2)}, u32[]{:S(2)}) async-start(bf16[32,24,384]{2,1,0:T(8,128)(2,1)} %bitcast.9), calls=%async_computation.1 | async-start | bytes 1179648 | tf_op jit(solution)/shard_map/all_to_all | solution.py:527
  184.0 1.6 copy-start.2
  185.6 4.9 %collective-permute-start.6 = (f32[8,384]{1,0:T(8,128)S(1)}, f32[8,384]{1,0:T(8,128)S(1)}, u32[]{:S(2)}, u32[]{:S(2)}) collective-permute-start(f32[8,384]{1,0:T(8,128)S(1)} %add.447), channel_id=1, source_target_pairs={{0,32},{32,64},{64,96},{96,128},{128,160},{160,192},{192,224},{224... | collective-permute-start | bytes 36872 | tf_op jit(solution)/shard_map/ppermute | solution.py:508
  188.1 0.9 copy-start.4
  201.5 54.5 %copy-start = (bf16[6,392,768]{2,1,0:T(8,128)(2,1)S(1)}, bf16[6,392,768]{2,1,0:T(8,128)(2,1)}, u32[]{:S(2)}) copy-start(bf16[6,392,768]{2,1,0:T(8,128)(2,1)} %get-tuple-element.23.table_ref) | copy-start | bytes 10838020
  262.0 5.5 %copy-start.7 = (bf16[1,192]{1,0:T(2,128)(2,1)S(1)}, bf16[1,192]{1,0:T(2,128)(2,1)}, u32[]{:S(2)}) copy-start(bf16[1,192]{1,0:T(2,128)(2,1)} %param.10) | copy-start | bytes 1156
  262.0 9.1 %copy-start.6 = (bf16[1,384]{1,0:T(2,128)(2,1)S(1)}, bf16[1,384]{1,0:T(2,128)(2,1)}, u32[]{:S(2)}) copy-start(bf16[1,384]{1,0:T(2,128)(2,1)} %param.12) | copy-start | bytes 2308
  262.0 88.1 %all-to-all-start.4 = ((bf16[32,144,384]{2,1,0:T(8,128)(2,1)}), bf16[32,144,384]{2,1,0:T(8,128)(2,1)S(1)}, u32[]{:S(2)}, u32[]{:S(2)}) async-start(bf16[32,144,384]{2,1,0:T(8,128)(2,1)} %bitcast.33), calls=%async_computation.4 | async-start | bytes 7077888 | tf_op jit(solution)/shard_map/all_to_all | solution.py:527
  267.5 45.0 %collective-permute-start.7 = (bf16[12,192,768]{2,1,0:T(8,128)(2,1)}, bf16[12,192,768]{2,1,0:T(8,128)(2,1)}, u32[]{:S(2)}, u32[]{:S(2)}) collective-permute-start(bf16[12,192,768]{2,1,0:T(8,128)(2,1)} %bitcast.39), channel_id=1, source_target_pairs={{0,32},{32,64},{64,96},{96,128},{128,160},{160,192},{192,224},{224... | collective-permute-start | bytes 10616840 | tf_op jit(solution)/shard_map/ppermute | solution.py:508
  267.5 41.2 %collective-permute-start.8 = (bf16[1,192]{1,0:T(2,128)(2,1)S(1)}, bf16[1,192]{1,0:T(2,128)(2,1)S(1)}, u32[]{:S(2)}, u32[]{:S(2)}) collective-permute-start(bf16[1,192]{1,0:T(2,128)(2,1)S(1)} %copy-done.7), channel_id=1, source_target_pairs={{0,32},{32,64},{64,96},{96,128},{128,160},{160,192},{192,224},{224... | collective-permute-start | bytes 1160 | tf_op jit(solution)/shard_map/ppermute | solution.py:508
  271.1 40.6 %collective-permute-start.9 = (bf16[1,192,384]{1,2,0:T(8,128)(2,1)}, bf16[1,192,384]{1,2,0:T(8,128)(2,1)}, u32[]{:S(2)}, u32[]{:S(2)}) collective-permute-start(bf16[1,192,384]{1,2,0:T(8,128)(2,1)} %copy.13), channel_id=1, source_target_pairs={{0,32},{32,64},{64,96},{96,128},{128,160},{160,192},{192,224},{224... | collective-permute-start | bytes 442376 | tf_op jit(solution)/shard_map/ppermute | solution.py:508
  271.1 39.7 %collective-permute-start.10 = (bf16[1,384]{1,0:T(2,128)(2,1)S(1)}, bf16[1,384]{1,0:T(2,128)(2,1)S(1)}, u32[]{:S(2)}, u32[]{:S(2)}) collective-permute-start(bf16[1,384]{1,0:T(2,128)(2,1)S(1)} %copy-done.6), channel_id=1, source_target_pairs={{0,32},{32,64},{64,96},{96,128},{128,160},{160,192},{192,224},{224... | collective-permute-start | bytes 2312 | tf_op jit(solution)/shard_map/ppermute | solution.py:508
  271.2 41.3 %collective-permute-start.11 = (bf16[1,192,384]{2,1,0:T(8,128)(2,1)}, bf16[1,192,384]{2,1,0:T(8,128)(2,1)}, u32[]{:S(2)}, u32[]{:S(2)}) collective-permute-start(bf16[1,192,384]{2,1,0:T(8,128)(2,1)} %param.13), channel_id=1, source_target_pairs={{0,32},{32,64},{64,96},{96,128},{128,160},{160,192},{192,224},{224... | collective-permute-start | bytes 442376 | tf_op jit(solution)/shard_map/ppermute | solution.py:508

commit v3 on v2

--- a/solution.py
+++ b/solution.py
@@ -22,6 +22,7 @@
 BLOCK_M = 2 * PAIRS * ROWS
 BLOCK_L = 2 * PAIRS * PAIRS
 EARLY = 2
+SWAPPED = 4
 T_ROWS = LMAX
 T_PAD = T_ROWS + 8
 LANES = 2 * NLAT
@@ -554,12 +555,12 @@
     field = field_in[0]
     rank = lax.axis_index("sp")
     weight = spectral_weight[0]
-    early_weight = to_next_mirrored(weight[PAIRS : PAIRS + 3])
+    early_weight = to_next_mirrored(weight[PAIRS : PAIRS + SWAPPED])
     spectral = analysis(rank.reshape(1), field, spectral_gain)
     rank_after, weight, _ = lax.optimization_barrier((rank, weight, spectral))
     by_order = exchange(spectral.reshape(SP, BLOCK_M, K2))
     own_weight = to_next(weight[:PAIRS])
-    late_weight = to_next(weight[PAIRS + 3 :])
+    late_weight = to_next(weight[PAIRS + SWAPPED :])
     legendre, table = legendre_table(*legendre_inputs(rank_after))
     first_choice = mixing_choice(rank_after, EARLY, PAIRS - EARLY)
     second_choice = mixing_choice(rank_after, 0, EARLY)

time: 366 us -> 370 us (1.011)
  waiting for transfers between devices: 172 us -> 180 us
    ppermute x1, waiting for transfers between devices: 0.41 us -> 22.3 us  [to_mirrored(): return lax.ppermute(value, 'sp', [(d, count - 1 - d) for d in range(count)])]
    ppermute x1, waiting for transfers between devices: 15.5 us -> 4.93 us  [to_next_mirrored(): return lax.ppermute(value, ('section', 'sp'), pairs)]
  transfers between devices with their start and end apart: 16 -> 16, of which waited for: 10 -> 8; matrix products, arithmetic and copies ran while one was open for 4% -> 3% of each run, Pallas kernels for 9% -> 9%
where the time goes in v3:
time: 370 us; the launch traced here: 369 us
  waiting for transfers between devices  180 us (49%)
  Pallas kernels  73.9 us (20%)
  starting transfers between devices  50.1 us (14%)
  blocking collectives  49.3 us (13%)
  local copies, waits for them, and re-layouts  11.2 us (3%)
  other arithmetic  4.39 us (1%)
    all_to_all x4, waiting for transfers between devices, exchange(): return lax.all_to_all(value, 'sp', split_axis=0, concat_axis=0)  113 us
    all_to_all x1, blocking collectives, exchange(): return lax.all_to_all(value, 'sp', split_axis=0, concat_axis=0)  49.3 us
    all_to_all x4, starting transfers between devices, exchange(): return lax.all_to_all(value, 'sp', split_axis=0, concat_axis=0)  40 us
    ppermute x10, waiting for transfers between devices, to_next(): lax.ppermute(value, 'section', [(i, (i + 1) % count) for i in range(count)])  39.8 us
    pallas_call x1, Pallas kernels, legendre_table(): pl.pallas_call(legendre_kernel, grid=(PAIRS,), in_specs=[whole((2, 8, 128...  23.9 us
    ppermute x1, waiting for transfers between devices, to_mirrored(): return lax.ppermute(value, 'sp', [(d, count - 1 - d) for d in range(count)])  22.3 us
    pallas_call x1, Pallas kernels, synthesis(): pl.pallas_call(synthesis_kernel, grid=(ROWS // 2,), in_specs=[IN_VMEM, cy...  13.7 us
    pallas_call x1, Pallas kernels, analysis(): pl.pallas_call(analysis_kernel, grid=(steps + 6,), in_specs=[pl.BlockSpec...  11.7 us
  transfers between devices with their start and end apart: 16, of which 8 were waited for; matrix products, arithmetic and copies ran while one was open for 3% of the time, Pallas kernels for 9%

profile of v3, /device:TPU:4, one launch (start us, length us, event | category | flops | bytes accessed | tf_op | source)
XLA Modules:
  0.0 368.8 jit_solution(10444572951388286783)
XLA Ops:
  0.7 11.7 %analysis.1 = bf16[4608,384]{1,0:T(8,128)(2,1)} custom-call(s32[1]{0:T(128)} %bitcast.1.rank_ref, bf16[12,192,768]{2,1,0:T(8,128)(2,1)} %bitcast.38, bf16[1,192]{1,0:T(2,128)(2,1)S(1)} %copy-done.3), custom_call_target="tpu_custom_call" | custom-call | flops 3600000000 | bytes 9000000 | tf_op jit(solution)/shard_map/analysis/pallas_call | solution.py:154
  12.4 11.5 %all-to-all-start = ((bf16[32,144,384]{2,1,0:T(8,128)(2,1)}), bf16[32,144,384]{2,1,0:T(8,128)(2,1)S(1)}, u32[]{:S(2)}, u32[]{:S(2)}) async-start(bf16[32,144,384]{2,1,0:T(8,128)(2,1)} %bitcast.34), calls=%async_computation | async-start | bytes 7077888 | tf_op jit(solution)/shard_map/all_to_all | solution.py:528
  24.8 23.9 %legendre_table.1 = (bf16[6,392,768]{2,1,0:T(8,128)(2,1)}, bf16[768,768]{1,0:T(8,128)(2,1)}) custom-call(f32[2,8,128]{2,1,0:T(8,128)S(1)} %broadcast_in_dim.76.orders_ref, f32[8,768]{1,0:T(8,128)S(1)} %broadcast_in_dim.77.cosine_ref, f32[8,768]{1,0:T(8,128)S(1)} %broadcast_in_dim.78.low_ref, f32[8,768]{1,0:T(8,128)S(1)} %add_multiply_fusion.start_ref), custom_call_target="tpu_custom_call" | custom-call | flops 10000000000 | bytes 4000000 | tf_op jit(solution)/shard_map/legendre_table/pallas_call | solution.py:265
  48.6 58.2 %all-to-all-done = bf16[32,144,384]{2,1,0:T(8,128)(2,1)S(1)} async-done(((bf16[32,144,384]{2,1,0:T(8,128)(2,1)}), bf16[32,144,384]{2,1,0:T(8,128)(2,1)S(1)}, u32[]{:S(2)}, u32[]{:S(2)}) %all-to-all-start) | async-done | bytes 3538976 | tf_op jit(solution)/shard_map/all_to_all | solution.py:528
  106.9 1.1 broadcast_in_dim.88.choice_ref
  108.0 0.9 broadcast_in_dim.89.choice_ref
  108.9 4.9 %forward.3 = (bf16[1536,384]{1,0:T(8,128)(2,1)}, f32[8,384]{1,0:T(8,128)S(1)}) custom-call(bf16[6,392,768]{2,1,0:T(8,128)(2,1)} %get-tuple-element.23.table_ref, bf16[32,6,24,384]{3,2,1,0:T(8,128)(2,1)S(1)} %bitcast.30), custom_call_target="tpu_custom_call" | custom-call | flops 920000000 | bytes 6000000 | tf_op jit(solution)/shard_map/forward/pallas_call | solution.py:305
  113.8 4.7 %all-to-all-start.2 = ((bf16[32,48,384]{2,1,0:T(8,128)(2,1)}), bf16[32,48,384]{2,1,0:T(8,128)(2,1)}, u32[]{:S(2)}, u32[]{:S(2)}) async-start(bf16[32,48,384]{2,1,0:T(8,128)(2,1)} %bitcast.37), calls=%async_computation.2 | async-start | bytes 2359296 | tf_op jit(solution)/shard_map/all_to_all | solution.py:528
  118.5 1.0 slice.40
  119.5 2.2 slice.41
  121.7 1.3 collective-permute-start.2
  123.0 3.0 forward.2
  126.6 1.1 slice_bitcast_fusion
  127.7 5.4 %collective-permute-start.3 = (bf16[4,192,384]{2,1,0:T(8,128)(2,1)S(1)}, bf16[4,192,384]{2,1,0:T(8,128)(2,1)S(1)}, u32[]{:S(2)}, u32[]{:S(2)}) collective-permute-start(bf16[4,192,384]{2,1,0:T(8,128)(2,1)S(1)} %slice_bitcast_fusion), channel_id=1, source_target_pairs={{0,63},{1,62},{2,61},{3,60},{4,59},{5,58},{6,57},{7,56},{8,55},{9,... | collective-permute-start | bytes 1769480 | tf_op jit(solution)/shard_map/ppermute | solution.py:524
  133.1 16.8 %all-to-all-done.2 = bf16[32,48,384]{2,1,0:T(8,128)(2,1)} async-done(((bf16[32,48,384]{2,1,0:T(8,128)(2,1)}), bf16[32,48,384]{2,1,0:T(8,128)(2,1)}, u32[]{:S(2)}, u32[]{:S(2)}) %all-to-all-start.2) | async-done | bytes 1179680 | tf_op jit(solution)/shard_map/all_to_all | solution.py:528
  149.9 18.4 %all-to-all-start.1 = ((bf16[32,24,384]{2,1,0:T(8,128)(2,1)}), bf16[32,24,384]{2,1,0:T(8,128)(2,1)}, u32[]{:S(2)}, u32[]{:S(2)}) async-start(bf16[32,24,384]{2,1,0:T(8,128)(2,1)} %bitcast.9), calls=%async_computation.1 | async-start | bytes 1179648 | tf_op jit(solution)/shard_map/all_to_all | solution.py:528
  168.3 4.9 %collective-permute-done.3 = bf16[4,192,384]{2,1,0:T(8,128)(2,1)S(1)} collective-permute-done((bf16[4,192,384]{2,1,0:T(8,128)(2,1)S(1)}, bf16[4,192,384]{2,1,0:T(8,128)(2,1)S(1)}, u32[]{:S(2)}, u32[]{:S(2)}) %collective-permute-start.3) | collective-permute-done | bytes 589856 | tf_op jit(solution)/shard_map/ppermute | solution.py:524
  174.1 1.5 slice_negate_fusion.1
  175.6 1.6 maximum_maximum_fusion.own_ref
  178.0 22.3 %collective-permute-done.4 = bf16[2,192,384]{2,1,0:T(8,128)(2,1)S(1)} collective-permute-done((bf16[2,192,384]{2,1,0:T(8,128)(2,1)}, bf16[2,192,384]{2,1,0:T(8,128)(2,1)S(1)}, u32[]{:S(2)}, u32[]{:S(2)}) %collective-permute-start.4) | collective-permute-done | bytes 294944 | tf_op jit(solution)/shard_map/ppermute | solution.py:514
  201.0 6.5 %mixing.2 = (bf16[32,72,384]{2,1,0:T(8,128)(2,1)}, f32[8,384]{1,0:T(8,128)S(1)}) custom-call(s32[1]{0:T(128)} %bitcast.1.rank_ref, bf16[32,48,384]{2,1,0:T(8,128)(2,1)} %collective-permute-done.5.coeffs_ref, f32[3,512,128]{2,1,0:T(8,128)} %broadcast_in_dim.88.choice_ref, bf16[6,384,384]{2,1,0:T(8,128)(2,1)S(1)} %maximum_maximum_fusion.own_ref, ...), custom_call_target="tpu_custom_call" | custom-call | flops 1800000000 | bytes 4800000 | tf_op jit(solution)/shard_map/mixing/pallas_call | solution.py:370
  207.5 4.2 %mixing.3 = (bf16[32,72,384]{2,1,0:T(8,128)(2,1)}, f32[8,384]{1,0:T(8,128)S(1)}) custom-call(s32[1]{0:T(128)} %bitcast.1.rank_ref, bf16[32,24,384]{2,1,0:T(8,128)(2,1)} %all-to-all-done.1.coeffs_ref, f32[3,256,128]{2,1,0:T(8,128)} %broadcast_in_dim.89.choice_ref, ...), custom_call_target="tpu_custom_call", output_to_operand_aliasing={{0}: (6, {})} | custom-call | flops 900000000 | bytes 2400000 | tf_op jit(solution)/shard_map/mixing/pallas_call | solution.py:370
  211.7 49.3 %all_to_all.25.mixed_ref = bf16[32,72,384]{2,1,0:T(8,128)(2,1)S(1)} all-to-all(bf16[32,72,384]{2,1,0:T(8,128)(2,1)} %get-tuple-element.36), channel_id=1, replica_groups=mesh['section'=8,'sp'=32] {'sp'}, dimensions={0} | all-to-all | bytes 3538944 | tf_op jit(solution)/shard_map/all_to_all | solution.py:528
  261.0 6.0 %inverse.1 = bf16[32,6,24,384]{3,2,1,0:T(8,128)(2,1)} custom-call(bf16[6,392,768]{2,1,0:T(8,128)(2,1)S(1)} %copy-done, bf16[32,72,384]{2,1,0:T(8,128)(2,1)S(1)} %all_to_all.25.mixed_ref, f32[8,384]{1,0:T(8,128)S(1)} %get-tuple-element.37.diag_ref), custom_call_target="tpu_custom_call" | custom-call | flops 1400000000 | bytes 9000000 | tf_op jit(solution)/shard_map/inverse/pallas_call | solution.py:430
  267.0 5.4 %all-to-all-start.4 = ((bf16[32,144,384]{2,1,0:T(8,128)(2,1)}), bf16[32,144,384]{2,1,0:T(8,128)(2,1)S(1)}, u32[]{:S(2)}, u32[]{:S(2)}) async-start(bf16[32,144,384]{2,1,0:T(8,128)(2,1)} %bitcast.33), calls=%async_computation.4 | async-start | bytes 7077888 | tf_op jit(solution)/shard_map/all_to_all | solution.py:528
  272.8 1.7 copy.13
  274.6 1.4 collective-permute-start.10
  276.0 37.7 %collective-permute-done.8 = bf16[1,192]{1,0:T(2,128)(2,1)S(1)} collective-permute-done((bf16[1,192]{1,0:T(2,128)(2,1)S(1)}, bf16[1,192]{1,0:T(2,128)(2,1)S(1)}, u32[]{:S(2)}, u32[]{:S(2)}) %collective-permute-start.8) | collective-permute-done | bytes 416 | tf_op jit(solution)/shard_map/ppermute | solution.py:509
  314.5 1.3 collective-permute-done.10
  315.8 0.8 copy.15.bias_ref
  317.4 37.7 %all-to-all-done.4 = bf16[32,144,384]{2,1,0:T(8,128)(2,1)S(1)} async-done(((bf16[32,144,384]{2,1,0:T(8,128)(2,1)}), bf16[32,144,384]{2,1,0:T(8,128)(2,1)S(1)}, u32[]{:S(2)}, u32[]{:S(2)}) %all-to-all-start.4) | async-done | bytes 3538976 | tf_op jit(solution)/shard_map/all_to_all | solution.py:528
  355.1 13.7 %synthesis.1 = bf16[12,192,768]{2,1,0:T(8,128)(2,1)} custom-call(bf16[4608,384]{1,0:T(8,128)(2,1)S(1)} %bitcast.32, bf16[12,192,768]{2,1,0:T(8,128)(2,1)} %collective-permute-done.7.field_ref, bf16[768,768]{1,0:T(8,128)(2,1)} %get-tuple-element.38.table_ref, f32[192,1]{1,0:T(8,128)} %copy.14.gain_ref, bf16[384,192]{1,0:T(8,128)(2,1)} %bitcast.16.up_ref, ...), custom_call_target="tpu_custom_call" | custom-call | flops 8000000000 | bytes 12000000 | tf_op jit(solution)/shard_map/synthesis/pallas_call | solution.py:479
  (62 shorter events, 6.5 us)
Async XLA Ops:
  0.0 0.7 copy-start.3
  12.4 94.4 %all-to-all-start = ((bf16[32,144,384]{2,1,0:T(8,128)(2,1)}), bf16[32,144,384]{2,1,0:T(8,128)(2,1)S(1)}, u32[]{:S(2)}, u32[]{:S(2)}) async-start(bf16[32,144,384]{2,1,0:T(8,128)(2,1)} %bitcast.34), calls=%async_computation | async-start | bytes 7077888 | tf_op jit(solution)/shard_map/all_to_all | solution.py:528
  113.8 36.1 %all-to-all-start.2 = ((bf16[32,48,384]{2,1,0:T(8,128)(2,1)}), bf16[32,48,384]{2,1,0:T(8,128)(2,1)}, u32[]{:S(2)}, u32[]{:S(2)}) async-start(bf16[32,48,384]{2,1,0:T(8,128)(2,1)} %bitcast.37), calls=%async_computation.2 | async-start | bytes 2359296 | tf_op jit(solution)/shard_map/all_to_all | solution.py:528
  119.5 7.1 %collective-permute-start = (bf16[2,192,384]{2,1,0:T(8,128)(2,1)S(1)}, bf16[2,192,384]{2,1,0:T(8,128)(2,1)}, u32[]{:S(2)}, u32[]{:S(2)}) collective-permute-start(bf16[2,192,384]{2,1,0:T(8,128)(2,1)S(1)} %slice.40), channel_id=1, source_target_pairs={{0,32},{32,64},{64,96},{96,128},{128,160},{160,192},{192,224},{224... | collective-permute-start | bytes 884744 | tf_op jit(solution)/shard_map/ppermute | solution.py:509
  121.7 52.4 %collective-permute-start.2 = (bf16[6,192,384]{2,1,0:T(8,128)(2,1)}, bf16[6,192,384]{2,1,0:T(8,128)(2,1)}, u32[]{:S(2)}, u32[]{:S(2)}) collective-permute-start(bf16[6,192,384]{2,1,0:T(8,128)(2,1)} %slice.41), channel_id=1, source_target_pairs={{0,32},{32,64},{64,96},{96,128},{128,160},{160,192},{192,224},{224... | collective-permute-start | bytes 2654216 | tf_op jit(solution)/shard_map/ppermute | solution.py:509
  126.0 0.6 copy-start.1
  126.6 23.3 %collective-permute-start.1 = (bf16[768,384]{1,0:T(8,128)(2,1)}, bf16[768,384]{1,0:T(8,128)(2,1)}, u32[]{:S(2)}, u32[]{:S(2)}) collective-permute-start(bf16[768,384]{1,0:T(8,128)(2,1)} %get-tuple-element.27), channel_id=1, source_target_pairs={{0,32},{32,64},{64,96},{96,128},{128,160},{160,192},{192,224},{224... | collective-permute-start | bytes 1769480 | tf_op jit(solution)/shard_map/ppermute | solution.py:509
  127.7 45.5 %collective-permute-start.3 = (bf16[4,192,384]{2,1,0:T(8,128)(2,1)S(1)}, bf16[4,192,384]{2,1,0:T(8,128)(2,1)S(1)}, u32[]{:S(2)}, u32[]{:S(2)}) collective-permute-start(bf16[4,192,384]{2,1,0:T(8,128)(2,1)S(1)} %slice_bitcast_fusion), channel_id=1, source_target_pairs={{0,63},{1,62},{2,61},{3,60},{4,59},{5,58},{6,57},{7,56},{8,55},{9,... | collective-permute-start | bytes 1769480 | tf_op jit(solution)/shard_map/ppermute | solution.py:524
  149.9 51.1 %collective-permute-start.5 = (bf16[32,48,384]{2,1,0:T(8,128)(2,1)}, bf16[32,48,384]{2,1,0:T(8,128)(2,1)}, u32[]{:S(2)}, u32[]{:S(2)}) collective-permute-start(bf16[32,48,384]{2,1,0:T(8,128)(2,1)} %all-to-all-done.2), channel_id=1, source_target_pairs={{0,32},{32,64},{64,96},{96,128},{128,160},{160,192},{192,224},{224... | collective-permute-start | bytes 3538952 | tf_op jit(solution)/shard_map/ppermute | solution.py:509
  149.9 57.6 %all-to-all-start.1 = ((bf16[32,24,384]{2,1,0:T(8,128)(2,1)}), bf16[32,24,384]{2,1,0:T(8,128)(2,1)}, u32[]{:S(2)}, u32[]{:S(2)}) async-start(bf16[32,24,384]{2,1,0:T(8,128)(2,1)} %bitcast.9), calls=%async_computation.1 | async-start | bytes 1179648 | tf_op jit(solution)/shard_map/all_to_all | solution.py:528
  173.3 27.0 %collective-permute-start.4 = (bf16[2,192,384]{2,1,0:T(8,128)(2,1)}, bf16[2,192,384]{2,1,0:T(8,128)(2,1)S(1)}, u32[]{:S(2)}, u32[]{:S(2)}) collective-permute-start(bf16[2,192,384]{2,1,0:T(8,128)(2,1)} %collective-permute-done), channel_id=1, source_target_pairs={{0,31},{1,30},{2,29},{3,28},{4,27},{5,26},{6,25},{7,24},{8,23},{9,... | collective-permute-start | bytes 884744 | tf_op jit(solution)/shard_map/ppermute | solution.py:514
  175.6 1.6 copy-start.2
  177.2 23.8 %collective-permute-start.6 = (f32[8,384]{1,0:T(8,128)S(1)}, f32[8,384]{1,0:T(8,128)S(1)}, u32[]{:S(2)}, u32[]{:S(2)}) collective-permute-start(f32[8,384]{1,0:T(8,128)S(1)} %add.447), channel_id=1, source_target_pairs={{0,32},{32,64},{64,96},{96,128},{128,160},{160,192},{192,224},{224... | collective-permute-start | bytes 36872 | tf_op jit(solution)/shard_map/ppermute | solution.py:509
  207.5 53.5 %copy-start = (bf16[6,392,768]{2,1,0:T(8,128)(2,1)S(1)}, bf16[6,392,768]{2,1,0:T(8,128)(2,1)}, u32[]{:S(2)}) copy-start(bf16[6,392,768]{2,1,0:T(8,128)(2,1)} %get-tuple-element.23.table_ref) | copy-start | bytes 10838020
  267.0 5.5 %copy-start.5 = (bf16[1,192]{1,0:T(2,128)(2,1)S(1)}, bf16[1,192]{1,0:T(2,128)(2,1)}, u32[]{:S(2)}) copy-start(bf16[1,192]{1,0:T(2,128)(2,1)} %param.10) | copy-start | bytes 1156
  267.0 7.6 %copy-start.4 = (bf16[1,384]{1,0:T(2,128)(2,1)S(1)}, bf16[1,384]{1,0:T(2,128)(2,1)}, u32[]{:S(2)}) copy-start(bf16[1,384]{1,0:T(2,128)(2,1)} %param.12) | copy-start | bytes 2308
  267.0 88.1 %all-to-all-start.4 = ((bf16[32,144,384]{2,1,0:T(8,128)(2,1)}), bf16[32,144,384]{2,1,0:T(8,128)(2,1)S(1)}, u32[]{:S(2)}, u32[]{:S(2)}) async-start(bf16[32,144,384]{2,1,0:T(8,128)(2,1)} %bitcast.33), calls=%async_computation.4 | async-start | bytes 7077888 | tf_op jit(solution)/shard_map/all_to_all | solution.py:528
  272.5 45.0 %collective-permute-start.7 = (bf16[12,192,768]{2,1,0:T(8,128)(2,1)}, bf16[12,192,768]{2,1,0:T(8,128)(2,1)}, u32[]{:S(2)}, u32[]{:S(2)}) collective-permute-start(bf16[12,192,768]{2,1,0:T(8,128)(2,1)} %bitcast.39), channel_id=1, source_target_pairs={{0,32},{32,64},{64,96},{96,128},{128,160},{160,192},{192,224},{224... | collective-permute-start | bytes 10616840 | tf_op jit(solution)/shard_map/ppermute | solution.py:509
  272.5 41.2 %collective-permute-start.8 = (bf16[1,192]{1,0:T(2,128)(2,1)S(1)}, bf16[1,192]{1,0:T(2,128)(2,1)S(1)}, u32[]{:S(2)}, u32[]{:S(2)}) collective-permute-start(bf16[1,192]{1,0:T(2,128)(2,1)S(1)} %copy-done.5), channel_id=1, source_target_pairs={{0,32},{32,64},{64,96},{96,128},{128,160},{160,192},{192,224},{224... | collective-permute-start | bytes 1160 | tf_op jit(solution)/shard_map/ppermute | solution.py:509
  274.6 42.1 %collective-permute-start.9 = (bf16[1,192,384]{1,2,0:T(8,128)(2,1)}, bf16[1,192,384]{1,2,0:T(8,128)(2,1)}, u32[]{:S(2)}, u32[]{:S(2)}) collective-permute-start(bf16[1,192,384]{1,2,0:T(8,128)(2,1)} %copy.13), channel_id=1, source_target_pairs={{0,32},{32,64},{64,96},{96,128},{128,160},{160,192},{192,224},{224... | collective-permute-start | bytes 442376 | tf_op jit(solution)/shard_map/ppermute | solution.py:509
  274.6 41.2 %collective-permute-start.10 = (bf16[1,384]{1,0:T(2,128)(2,1)S(1)}, bf16[1,384]{1,0:T(2,128)(2,1)S(1)}, u32[]{:S(2)}, u32[]{:S(2)}) collective-permute-start(bf16[1,384]{1,0:T(2,128)(2,1)S(1)} %copy-done.4), channel_id=1, source_target_pairs={{0,32},{32,64},{64,96},{96,128},{128,160},{160,192},{192,224},{224... | collective-permute-start | bytes 2312 | tf_op jit(solution)/shard_map/ppermute | solution.py:509
  276.0 41.4 %collective-permute-start.11 = (bf16[1,192,384]{2,1,0:T(8,128)(2,1)}, bf16[1,192,384]{2,1,0:T(8,128)(2,1)}, u32[]{:S(2)}, u32[]{:S(2)}) collective-permute-start(bf16[1,192,384]{2,1,0:T(8,128)(2,1)} %param.13), channel_id=1, source_target_pairs={{0,32},{32,64},{64,96},{96,128},{128,160},{160,192},{192,224},{224... | collective-permute-start | bytes 442376 | tf_op jit(solution)/shard_map/ppermute | solution.py:509
